TPU v7x, 8 devices: a whole 2x2x1 slice. The times are simulated.
8 devices in a mesh: sp: 8 (over z, y, x, core).
Axes of the slice: x: 2, y: 2, z: 1, core: 2. Of those that a mesh axis runs over, the one named last changes fastest.
Arguments:
- x: bfloat16 [4096, 2048], P('sp')
- seg_ids: int32 [4096], P('sp')
- positions: int32 [4096], P('sp')
- grad_y: bfloat16 [4096, 2048], P('sp')
- norm1_gain: bfloat16 [2048], P('sp')
- w_q: bfloat16 [2048, 16, 128], P('sp')
- w_k: bfloat16 [2048, 16, 128], P('sp')
- w_v: bfloat16 [2048, 16, 128], P('sp')
- w_o: bfloat16 [16, 128, 2048], P('sp')
- norm2_gain: bfloat16 [2048], P('sp')
- w_gate: bfloat16 [2048, 5504], P('sp')
- w_up: bfloat16 [2048, 5504], P('sp')
- w_down: bfloat16 [5504, 2048], P('sp')
Outputs:
- output 1: bfloat16 [4096, 2048], P('sp')
- output 2: bfloat16 [4096, 2048], P('sp')
- output 3: float32 [2048], P('sp')
- output 4: float32 [2048, 16, 128], P('sp')
- output 5: float32 [2048, 16, 128], P('sp')
- output 6: float32 [2048, 16, 128], P('sp')
- output 7: float32 [16, 128, 2048], P('sp')
- output 8: float32 [2048], P('sp')
- output 9: float32 [2048, 5504], P('sp')
- output 10: float32 [2048, 5504], P('sp')
- output 11: float32 [5504, 2048], P('sp')
All inputs are finite; a program needn't handle non-finite values.
Results may differ from a plain program's by a relative error of at most 0.0156151.
Values are sent between devices in bfloat16 or wider.
A program may use at most 1 GiB of HBM per device.

v0:
```python
import jax
import jax.numpy as jnp
from jax import lax
from jax.sharding import PartitionSpec as P

NORM_EPS = 1e-5
ROPE_BASE = 10000.0
BLOCK = 256


def rope_tables(positions, head_dim):
    half = head_dim // 2
    inv_freq = ROPE_BASE ** (-jnp.arange(half, dtype=jnp.float32) * 2.0 / head_dim)
    angle = positions.astype(jnp.float32)[:, None] * inv_freq[None, :]
    cos_t = jnp.cos(angle)
    sin_t = jnp.sin(angle)
    cos_full = jnp.concatenate([cos_t, cos_t], axis=-1)[:, None, :]
    sin_full = jnp.concatenate([sin_t, sin_t], axis=-1)[:, None, :]
    return cos_full, sin_full


def rotate_half(t):
    half = t.shape[-1] // 2
    return jnp.concatenate([-t[..., half:], t[..., :half]], axis=-1)


def rope_apply(t, cos_full, sin_full):
    return t * cos_full + rotate_half(t) * sin_full


def rope_back(grad_in, cos_full, sin_full):
    return grad_in * cos_full - rotate_half(grad_in) * sin_full


def rms_back(grad_out, normed, inv_rms):
    mean_term = jnp.mean(grad_out * normed, axis=-1, keepdims=True)
    return inv_rms * (grad_out - normed * mean_term)


def block_mask(all_seg, q_start, rows):
    q_index = q_start + jnp.arange(rows)
    q_seg = lax.dynamic_slice(all_seg, (q_start,), (rows,))
    key_index = jnp.arange(all_seg.shape[0])
    return (key_index[None, :] <= q_index[:, None]) & (all_seg[None, :] == q_seg[:, None])


def block_probs(q_block, k_all, allowed):
    scale = k_all.shape[-1] ** -0.5
    logits = jnp.einsum('qgrd,kgd->grqk', q_block, k_all, preferred_element_type=jnp.float32) * scale
    return jax.nn.softmax(jnp.where(allowed, logits, -1e30), axis=-1)


def attn_forward(q_part, q_offset, k_all, v_all, all_seg):
    kv_count = k_all.shape[1]
    head_dim = k_all.shape[2]
    rows = q_part.shape[0]
    group = q_part.shape[1] // kv_count
    blk_rows = min(BLOCK, rows)
    num_blocks = rows // blk_rows
    q_blocks = q_part.reshape(num_blocks, blk_rows, kv_count, group, head_dim)

    def one_block(block_args):
        q_block, block_id = block_args
        allowed = block_mask(all_seg, q_offset + block_id * blk_rows, blk_rows)
        attn_probs = block_probs(q_block, k_all, allowed)
        return jnp.einsum('grqk,kgd->qgrd', attn_probs.astype(jnp.bfloat16), v_all,
                          preferred_element_type=jnp.float32).astype(jnp.bfloat16)

    attended = lax.map(one_block, (q_blocks, jnp.arange(num_blocks)))
    return attended.reshape(rows, kv_count * group, head_dim)


def attn_backward(q_part, q_offset, k_all, v_all, all_seg, grad_o):
    kv_count = k_all.shape[1]
    head_dim = k_all.shape[2]
    rows = q_part.shape[0]
    group = q_part.shape[1] // kv_count
    blk_rows = min(BLOCK, rows)
    num_blocks = rows // blk_rows
    scale = head_dim ** -0.5
    q_blocks = q_part.reshape(num_blocks, blk_rows, kv_count, group, head_dim)
    go_blocks = grad_o.reshape(num_blocks, blk_rows, kv_count, group, head_dim)

    def step(carry, block_args):
        dk_acc, dv_acc = carry
        q_block, go_block, block_id = block_args
        allowed = block_mask(all_seg, q_offset + block_id * blk_rows, blk_rows)
        attn_probs = block_probs(q_block, k_all, allowed)
        dv_acc = dv_acc + jnp.einsum('grqk,qgrd->kgd', attn_probs.astype(jnp.bfloat16), go_block,
                                     preferred_element_type=jnp.float32)
        grad_p = jnp.einsum('qgrd,kgd->grqk', go_block, v_all, preferred_element_type=jnp.float32)
        grad_p = grad_p.astype(jnp.bfloat16).astype(jnp.float32)
        delta = jnp.sum(attn_probs * grad_p, axis=-1, keepdims=True)
        grad_s = (attn_probs * (grad_p - delta) * scale).astype(jnp.bfloat16)
        dq_block = jnp.einsum('grqk,kgd->qgrd', grad_s, k_all, preferred_element_type=jnp.float32).astype(jnp.bfloat16)
        dk_acc = dk_acc + jnp.einsum('grqk,qgrd->kgd', grad_s, q_block, preferred_element_type=jnp.float32)
        return (dk_acc, dv_acc), dq_block

    zeros = jnp.zeros(k_all.shape, jnp.float32)
    (dk_acc, dv_acc), dq_blocks = lax.scan(step, (zeros, zeros), (q_blocks, go_blocks, jnp.arange(num_blocks)))
    return dq_blocks.reshape(rows, kv_count * group, head_dim), dk_acc, dv_acc


def solution(mesh):
    row_spec = P('sp', None)
    cube_spec = P('sp', None, None)
    vec_spec = P('sp')

    def gather(t):
        return lax.all_gather(t, 'sp', axis=0, tiled=True)

    def scatter_sum(t):
        return lax.psum_scatter(t, 'sp', scatter_dimension=0, tiled=True)

    def heads_to_seq(t):
        return lax.all_to_all(t, 'sp', 1, 0, tiled=True)

    def seq_to_heads(t):
        return lax.all_to_all(t, 'sp', 0, 1, tiled=True)

    def local_layer(x, seg_ids, positions, grad_y, norm1_gain, w_q, w_k, w_v, w_o, norm2_gain, w_gate, w_up, w_down):
        all_seg = gather(seg_ids)
        gain1 = gather(norm1_gain).astype(jnp.float32)
        wq_full = gather(w_q)
        wk_full = gather(w_k)
        wv_full = gather(w_v)
        x_wide = x.astype(jnp.float32)
        inv_rms1 = lax.rsqrt(jnp.mean(x_wide * x_wide, axis=-1, keepdims=True) + NORM_EPS)
        normed1 = x_wide * inv_rms1
        u_norm = (normed1 * gain1).astype(jnp.bfloat16)
        cos_full, sin_full = rope_tables(positions, w_q.shape[2])
        q_loc = rope_apply(jnp.einsum('td,dhe->the', u_norm, wq_full, preferred_element_type=jnp.float32),
                           cos_full, sin_full).astype(jnp.bfloat16)
        k_loc = rope_apply(jnp.einsum('td,dhe->the', u_norm, wk_full, preferred_element_type=jnp.float32),
                           cos_full, sin_full).astype(jnp.bfloat16)
        v_loc = jnp.einsum('td,dhe->the', u_norm, wv_full, preferred_element_type=jnp.float32).astype(jnp.bfloat16)
        q_all = heads_to_seq(q_loc)
        k_all = heads_to_seq(k_loc)
        v_all = heads_to_seq(v_loc)
        o_loc = seq_to_heads(attn_forward(q_all, 0, k_all, v_all, all_seg))
        wo_full = gather(w_o)
        h_res = (x_wide + jnp.einsum('the,hed->td', o_loc, wo_full, preferred_element_type=jnp.float32)).astype(jnp.bfloat16)
        h_wide = h_res.astype(jnp.float32)
        gain2 = gather(norm2_gain).astype(jnp.float32)
        inv_rms2 = lax.rsqrt(jnp.mean(h_wide * h_wide, axis=-1, keepdims=True) + NORM_EPS)
        normed2 = h_wide * inv_rms2
        z_norm = (normed2 * gain2).astype(jnp.bfloat16)
        wg_full = gather(w_gate)
        wu_full = gather(w_up)
        wd_full = gather(w_down)
        gate_pre = jnp.dot(z_norm, wg_full, preferred_element_type=jnp.float32)
        up_pre = jnp.dot(z_norm, wu_full, preferred_element_type=jnp.float32)
        gate_sig = jax.nn.sigmoid(gate_pre)
        gate_act = gate_pre * gate_sig
        mlp_act = (gate_act * up_pre).astype(jnp.bfloat16)
        y = (h_wide + jnp.dot(mlp_act, wd_full, preferred_element_type=jnp.float32)).astype(jnp.bfloat16)

        wd_back = gather(w_down)
        grad_act = jnp.einsum('td,fd->tf', grad_y, wd_back, preferred_element_type=jnp.float32)
        grad_act = grad_act.astype(jnp.bfloat16).astype(jnp.float32)
        grad_wdown = jnp.einsum('tf,td->fd', mlp_act, grad_y, preferred_element_type=jnp.float32)
        grad_gate = (grad_act * up_pre * gate_sig * (1.0 + gate_pre * (1.0 - gate_sig))).astype(jnp.bfloat16)
        grad_up = (grad_act * gate_act).astype(jnp.bfloat16)
        grad_wgate = jnp.einsum('td,tf->df', z_norm, grad_gate, preferred_element_type=jnp.float32)
        grad_wup = jnp.einsum('td,tf->df', z_norm, grad_up, preferred_element_type=jnp.float32)
        wg_back = gather(w_gate)
        wu_back = gather(w_up)
        grad_z = (jnp.einsum('tf,df->td', grad_gate, wg_back, preferred_element_type=jnp.float32)
                  + jnp.einsum('tf,df->td', grad_up, wu_back, preferred_element_type=jnp.float32))
        grad_z = grad_z.astype(jnp.bfloat16).astype(jnp.float32)
        gain2_back = gather(norm2_gain).astype(jnp.float32)
        grad_gain2 = jnp.sum(grad_z * normed2, axis=0)
        grad_h = (grad_y.astype(jnp.float32) + rms_back(grad_z * gain2_back, normed2, inv_rms2)).astype(jnp.bfloat16)
        grad_wo = jnp.einsum('the,td->hed', o_loc, grad_h, preferred_element_type=jnp.float32)
        wo_back = gather(w_o)
        grad_o = jnp.einsum('td,hed->the', grad_h, wo_back, preferred_element_type=jnp.float32).astype(jnp.bfloat16)
        dq_all, dk_sum, dv_sum = attn_backward(q_all, 0, k_all, v_all, all_seg, heads_to_seq(grad_o))
        dq_loc = seq_to_heads(dq_all)
        dk_loc = seq_to_heads(dk_sum.astype(jnp.bfloat16))
        dv_loc = seq_to_heads(dv_sum.astype(jnp.bfloat16))
        dq_pre = rope_back(dq_loc.astype(jnp.float32), cos_full, sin_full).astype(jnp.bfloat16)
        dk_pre = rope_back(dk_loc.astype(jnp.float32), cos_full, sin_full).astype(jnp.bfloat16)
        grad_wq = jnp.einsum('td,the->dhe', u_norm, dq_pre, preferred_element_type=jnp.float32)
        grad_wk = jnp.einsum('td,the->dhe', u_norm, dk_pre, preferred_element_type=jnp.float32)
        grad_wv = jnp.einsum('td,the->dhe', u_norm, dv_loc, preferred_element_type=jnp.float32)
        wq_back = gather(w_q)
        wk_back = gather(w_k)
        wv_back = gather(w_v)
        grad_u = (jnp.einsum('the,dhe->td', dq_pre, wq_back, preferred_element_type=jnp.float32)
                  + jnp.einsum('the,dhe->td', dk_pre, wk_back, preferred_element_type=jnp.float32)
                  + jnp.einsum('the,dhe->td', dv_loc, wv_back, preferred_element_type=jnp.float32))
        grad_u = grad_u.astype(jnp.bfloat16).astype(jnp.float32)
        gain1_back = gather(norm1_gain).astype(jnp.float32)
        grad_gain1 = jnp.sum(grad_u * normed1, axis=0)
        grad_x = (grad_h.astype(jnp.float32) + rms_back(grad_u * gain1_back, normed1, inv_rms1)).astype(jnp.bfloat16)
        return (y, grad_x, scatter_sum(grad_gain1), scatter_sum(grad_wq), scatter_sum(grad_wk),
                scatter_sum(grad_wv), scatter_sum(grad_wo), scatter_sum(grad_gain2), scatter_sum(grad_wgate),
                scatter_sum(grad_wup), scatter_sum(grad_wdown))

    return jax.shard_map(
        local_layer, mesh=mesh,
        in_specs=(row_spec, vec_spec, vec_spec, row_spec, vec_spec, cube_spec, cube_spec, cube_spec, cube_spec,
                  vec_spec, row_spec, row_spec, row_spec),
        out_specs=(row_spec, row_spec, vec_spec, cube_spec, cube_spec, cube_spec, cube_spec, vec_spec,
                   row_spec, row_spec, row_spec),
        check_vma=False)
```

profile of v0, /device:TPU:0, one launch (start us, length us, event | category | flops | bytes accessed | tf_op | source)
XLA Modules:
  0.0 2542.1 jit_solution(14684663354216688755)
XLA Ops:
  15.3 13.7 all-gather.1
  30.2 33.1 %all-gather.13.cloned.1.call-done = bf16[2048,16,128]{0,2,1:T(8,128)(2,1)} async-done(((bf16[256,16,128]{0,2,1:T(8,128)(2,1)}), bf16[2048,16,128]{0,2,1:T(8,128)(2,1)}) %all-gather.13.cloned.1.call-update) | async-done | bytes 8388624 | tf_op jit(solution)/shard_map/all_gather | solution.py:110
  63.4 7.1 fusion.114
  75.0 40.7 %all-gather.11.cloned.1.call-done = bf16[2048,16,128]{0,2,1:T(8,128)(2,1)} async-done(((bf16[256,16,128]{0,2,1:T(8,128)(2,1)}), bf16[2048,16,128]{0,2,1:T(8,128)(2,1)}) %all-gather.11.cloned.1.call-update) | async-done | bytes 8388624 | tf_op jit(solution)/shard_map/all_gather | solution.py:110
  115.7 7.1 fusion.116
  129.8 40.3 %all_to_all.120 = bf16[512,16,128]{0,2,1:T(8,128)(2,1)} all-to-all(bf16[512,16,128]{0,2,1:T(8,128)(2,1)S(1)} %get-tuple-element.265), channel_id=1, replica_groups=mesh['sp'=8] {'sp'}, dimensions={1} | all-to-all | bytes 4194304 | tf_op jit(solution)/shard_map/all_to_all | solution.py:116
  173.2 23.0 all-gather.15.cloned.1.call-done
  196.2 9.2 fusion.96
  205.5 7.1 all-to-all-start.2
  213.3 37.4 %all-gather = s32[8,1,512]{2,1,0:T(1,128)S(1)} all-gather(s32[1,1,512]{2,1,0:T(1,128)S(1)} %bitcast.280), channel_id=1, replica_groups=mesh['sp'=8] {'sp'}, dimensions={0}, use_global_device_ids=true | all-gather | bytes 18432 | tf_op jit(solution)/shard_map/all_gather | solution.py:110
  264.1 153.5 %while.25 = (s32[]{:T(128)}, bf16[16,256,2,1,128]{4,1,0,2,3:T(8,128)(2,1)}, s32[16]{0:T(128)S(1)}, s32[4096]{0:T(1024)S(1)}, bf16[16,256,2,1,128]{4,1,2,3,0:T(8,...) while((s32[]{:T(128)}, ...), condition=%wide.region_4.5_spmd, body=%wide.region_1.4_spmd.sunk | while | flops 1093729536 | bytes 40139992 | solution.py:69
  427.0 53.6 %all-gather.2 = bf16[8,1,256]{2,1,0:T(2,128)(2,1)S(1)} all-gather(bf16[1,1,256]{2,1,0:T(2,128)(2,1)S(1)} %reshape.174), channel_id=1, replica_groups=mesh['sp'=8] {'sp'}, dimensions={0}, use_global_device_ids=true | all-gather | bytes 4608 | tf_op jit(solution)/shard_map/all_gather | solution.py:110
  482.7 9.0 fusion.73
  491.8 19.8 fusion.108
  513.8 18.1 convolution_convert_fusion.2
  532.0 92.2 %all-gather.21.cloned.1.call-done = bf16[2048,5504]{1,0:T(8,128)(2,1)} async-done(((bf16[256,5504]{1,0:T(8,128)(2,1)}), bf16[2048,5504]{1,0:T(8,128)(2,1)}) %all-gather.21.cloned.1.call-update) | async-done | bytes 22544400 | tf_op jit(solution)/shard_map/all_gather | solution.py:110
  624.2 25.6 %fusion.46 = (bf16[512,5504]{1,0:T(8,128)(2,1)}, bf16[512,5504]{1,0:T(8,128)(2,1)}) fusion(bf16[512,5504]{1,0:T(8,128)(2,1)} %convolution_convert_fusion.2, f32[512,5504]{1,0:T(8,128)} %fusion.108, bf16[2048,5504]{1,0:T(8,128)(2,1)} %all-gather.21.cloned.1.call-done, bf16[512,2048]{1,0:T(8,128)(2,1)} %get-tuple-element.269, f32[2048]{0:T(1024)S(1)} %bitcast.275, ...), kind=kOutput, calls=%fused_computation.56 | convolution fusion | flops 11586371584 | bytes 52832256 | tf_op jit(solution)/shard_map/dot_general | solution.py:152
  649.7 19.4 fusion.122
  669.1 24.1 fusion.72
  698.3 7.9 fusion.99
  709.5 26.5 %all-to-all-done.4 = bf16[512,16,128]{2,0,1:T(8,128)(2,1)} async-done(((bf16[512,16,128]{2,0,1:T(8,128)(2,1)}), bf16[512,16,128]{2,0,1:T(8,128)(2,1)}, u32[]{:S(2)}, u32[]{:S(2)}) %all-to-all-start.4) | async-done | bytes 2097184 | tf_op jit(solution)/shard_map/all_to_all | solution.py:116
  740.9 492.6 %while.26 = (s32[]{:T(128)}, f32[4096,2,128]{0,2,1:T(8,128)}, f32[4096,2,128]{0,2,1:T(8,128)}, bf16[16,256,2,1,128]{4,1,0,2,3:T(8,128)(2,1)}, bf16[16,256,2,1,12...) while((s32[]{:T(128)}, f32[4096,2,128]{0,2,1:T(8,128)}, ...), condition=%wide.region_11.12_spmd.clone, body=%wide.region_7.11_spmd.clone.sunk | while | flops 2735799040 | bytes 214609312 | solution.py:100
  787.4 6.7 fusion.204
  818.3 6.7 fusion.204
  849.1 6.7 fusion.204
  880.0 6.7 fusion.204
  1241.6 6.8 copy.99
  1248.4 19.7 all-to-all-done.5
  1286.7 11.8 all-to-all-done.6
  1313.3 8.4 fusion.92
  1321.8 9.6 fusion.90
  1331.5 6.8 copy.103
  1338.3 42.0 %all_to_all.121 = bf16[4096,2,128]{2,1,0:T(2,128)(2,1)S(1)} all-to-all(bf16[4096,2,128]{2,1,0:T(2,128)(2,1)} %copy.103), channel_id=1, replica_groups=mesh['sp'=8] {'sp'}, dimensions={0} | all-to-all | bytes 4194304 | tf_op jit(solution)/shard_map/all_to_all | solution.py:119
  1382.1 8.2 fusion.88
  1391.9 9.8 fusion.84
  1402.4 23.5 fusion.104
  1425.9 25.2 fusion.102
  1451.4 23.5 fusion.125
  1475.0 19.5 fusion.74
  1494.5 9.6 fusion.124
  1504.1 9.9 fusion.123
  1513.9 10.9 fusion.67
  1524.9 23.1 all-reduce.2
  1562.5 100.6 %reduce-scatter.12.cloned.1.call-done = f32[256,16,128]{2,0,1:T(8,128)} async-done(((f32[2048,16,128]{2,0,1:T(8,128)}), f32[256,16,128]{2,0,1:T(8,128)}) %reduce-scatter.12.cloned.1.call-update) | async-done | bytes 2097168 | tf_op jit(solution)/shard_map/reduce_scatter | solution.py:113
  1667.2 106.9 %reduce-scatter.14.cloned.1.call-done = f32[2,128,2048]{2,1,0:T(8,128)} async-done(((f32[16,128,2048]{2,1,0:T(8,128)}), f32[2,128,2048]{2,1,0:T(8,128)}) %reduce-scatter.14.cloned.1.call-update) | async-done | bytes 2097168 | tf_op jit(solution)/shard_map/reduce_scatter | solution.py:113
  1774.1 253.7 %reduce-scatter.16.cloned.1.call-done = f32[256,5504]{1,0:T(8,128)} async-done(((f32[2048,5504]{1,0:T(8,128)}), f32[256,5504]{1,0:T(8,128)}) %reduce-scatter.16.cloned.1.call-update) | async-done | bytes 5636112 | tf_op jit(solution)/shard_map/reduce_scatter | solution.py:113
  2027.8 253.8 %reduce-scatter.18.cloned.1.call-done = f32[256,5504]{1,0:T(8,128)} async-done(((f32[2048,5504]{1,0:T(8,128)}), f32[256,5504]{1,0:T(8,128)}) %reduce-scatter.18.cloned.1.call-update) | async-done | bytes 5636112 | tf_op jit(solution)/shard_map/reduce_scatter | solution.py:113
  2281.6 253.7 %reduce-scatter.20.cloned.1.call-done = f32[688,2048]{1,0:T(8,128)} async-done(((f32[5504,2048]{1,0:T(8,128)}), f32[688,2048]{1,0:T(8,128)}) %reduce-scatter.20.cloned.1.call-update) | async-done | bytes 5636112 | tf_op jit(solution)/shard_map/reduce_scatter | solution.py:113
  (682 shorter events, 726.0 us)
Async XLA Ops:
  7.2 56.2 %all-gather.13.cloned.1.call-start = ((), (), s32[]{:S(2)}) async-start(), calls=%async_computation.16 | async-start | bytes 9437184 | tf_op jit(solution)/shard_map/all_gather | solution.py:110
  9.7 106.0 %all-gather.11.cloned.1.call-start = ((), (), s32[]{:S(2)}) async-start(), calls=%async_computation.15 | async-start | bytes 9437184 | tf_op jit(solution)/shard_map/all_gather | solution.py:110
  12.2 184.0 %all-gather.15.cloned.1.call-start = ((), (), s32[]{:S(2)}) async-start(), calls=%async_computation.17 | async-start | bytes 9437184 | tf_op jit(solution)/shard_map/all_gather | solution.py:110
  13.5 15.5 copy-start.46
  13.5 16.2 copy-start.12
  13.6 469.1 %all-gather.17.cloned.1.call-start = ((), (), s32[]{:S(2)}) async-start(), calls=%async_computation.18 | async-start | bytes 9437184 | tf_op jit(solution)/shard_map/all_gather | solution.py:110
  14.1 477.6 %all-gather.19.cloned.1.call-start = ((), (), s32[]{:S(2)}) async-start(), calls=%async_computation.19 | async-start | bytes 25362432 | tf_op jit(solution)/shard_map/all_gather | solution.py:110
  14.7 499.1 %all-gather.23.cloned.1.call-start = ((), (), s32[]{:S(2)}) async-start(), calls=%async_computation.21 | async-start | bytes 25362432 | tf_op jit(solution)/shard_map/all_gather | solution.py:110
  29.1 167.2 %copy-start.36 = (f32[8,1,256]{2,1,0:T(1,128)}, f32[8,1,256]{2,1,0:T(1,128)S(1)}, u32[]{:S(2)}) copy-start(f32[8,1,256]{2,1,0:T(1,128)S(1)} %convert_element_type.214) | copy-start | bytes 24580
  29.7 93.9 %copy-start.21 = (f32[512,128]{0,1:T(8,128)}, f32[512,128]{0,1:T(8,128)S(1)}, u32[]{:S(2)}) copy-start(f32[512,128]{0,1:T(8,128)S(1)} %get-tuple-element.272) | copy-start | bytes 786436
  29.7 93.9 %copy-start.23 = (f32[512,128]{0,1:T(8,128)}, f32[512,128]{0,1:T(8,128)S(1)}, u32[]{:S(2)}) copy-start(f32[512,128]{0,1:T(8,128)S(1)} %get-tuple-element.273) | copy-start | bytes 786436
  30.2 166.0 %copy-start.40 = (f32[512]{0:T(512)}, f32[512]{0:T(512)S(1)}, u32[]{:S(2)}) copy-start(f32[512]{0:T(512)S(1)} %add_rsqrt_fusion.1) | copy-start | bytes 6148
  170.1 35.3 %all-to-all-start.1 = ((bf16[512,16,128]{0,2,1:T(8,128)(2,1)}), bf16[512,16,128]{0,2,1:T(8,128)(2,1)}, u32[]{:S(2)}, u32[]{:S(2)}) async-start(bf16[512,16,128]{0,2,1:T(8,128)(2,1)} %get-tuple-element.264), calls=%async_computation.1 | async-start | bytes 4194304 | tf_op jit(solution)/shard_map/all_to_all | solution.py:116
  205.5 45.2 %copy-start.15 = (bf16[512,16,128]{0,2,1:T(8,128)(2,1)S(1)}, bf16[512,16,128]{0,2,1:T(8,128)(2,1)}, u32[]{:S(2)}) copy-start(bf16[512,16,128]{0,2,1:T(8,128)(2,1)} %all_to_all.120) | copy-start | bytes 6291460
  205.5 53.8 %all-to-all-start.2 = ((bf16[512,16,128]{2,0,1:T(8,128)(2,1)}), bf16[512,16,128]{2,0,1:T(8,128)(2,1)}, u32[]{:S(2)}, u32[]{:S(2)}) async-start(bf16[512,16,128]{2,0,1:T(8,128)(2,1)} %fusion.96), calls=%async_computation.2 | async-start | bytes 4194304 | tf_op jit(solution)/shard_map/all_to_all | solution.py:116
  212.5 411.7 %all-gather.21.cloned.1.call-start = ((), (), s32[]{:S(2)}) async-start(), calls=%async_computation.20 | async-start | bytes 25362432 | tf_op jit(solution)/shard_map/all_gather | solution.py:110
  417.7 9.3 copy-start.48
  423.9 56.7 %all-to-all-start.3 = ((bf16[4096,2,128]{2,1,0:T(2,128)(2,1)}), bf16[4096,2,128]{2,1,0:T(2,128)(2,1)}, u32[]{:S(2)}, u32[]{:S(2)}) async-start(bf16[4096,2,128]{2,1,0:T(2,128)(2,1)} %copy.87), calls=%async_computation.3 | async-start | bytes 4194304 | tf_op jit(solution)/shard_map/all_to_all | solution.py:119
  480.6 212.7 %copy-start.38 = (f32[8,1,256]{2,1,0:T(1,128)}, f32[8,1,256]{2,1,0:T(1,128)S(1)}, u32[]{:S(2)}) copy-start(f32[8,1,256]{2,1,0:T(1,128)S(1)} %convert_element_type.215) | copy-start | bytes 24580
  482.6 9.1 copy-start.11
  491.7 201.6 %copy-start.42 = (f32[512]{0:T(512)}, f32[512]{0:T(512)S(1)}, u32[]{:S(2)}) copy-start(f32[512]{0:T(512)S(1)} %add_rsqrt_fusion) | copy-start | bytes 6148
  491.8 22.1 copy-start.27
  706.2 29.8 %all-to-all-start.4 = ((bf16[512,16,128]{2,0,1:T(8,128)(2,1)}), bf16[512,16,128]{2,0,1:T(8,128)(2,1)}, u32[]{:S(2)}, u32[]{:S(2)}) async-start(bf16[512,16,128]{2,0,1:T(8,128)(2,1)} %fusion.99), calls=%async_computation.4 | async-start | bytes 4194304 | tf_op jit(solution)/shard_map/all_to_all | solution.py:116
  709.4 31.4 %copy-start.4 = (bf16[4096,2,128]{2,0,1:T(8,128)(2,1)S(1)}, bf16[4096,2,128]{2,0,1:T(8,128)(2,1)}, u32[]{:S(2)}) copy-start(bf16[4096,2,128]{2,0,1:T(8,128)(2,1)} %copy-done.3) | copy-start | bytes 6291460
  709.4 31.4 %copy-start.26 = (s32[4096]{0:T(1024)S(1)}, s32[4096]{0:T(1024)}, u32[]{:S(2)}) copy-start(s32[4096]{0:T(1024)} %copy-done.25) | copy-start | bytes 49156
  787.4 8.6 copy-start.19
  818.3 8.6 copy-start.19
  849.1 8.6 copy-start.19
  880.0 8.6 copy-start.19
  910.9 8.6 copy-start.19
  941.7 8.6 copy-start.19
  972.6 8.6 copy-start.19
  1034.3 8.6 copy-start.19
  1065.2 8.6 copy-start.19
  1239.2 28.9 %all-to-all-start.5 = ((bf16[4096,2,128]{2,1,0:T(2,128)(2,1)}), bf16[4096,2,128]{2,1,0:T(2,128)(2,1)S(1)}, u32[]{:S(2)}, u32[]{:S(2)}) async-start(bf16[4096,2,128]{2,1,0:T(2,128)(2,1)} %copy.94), calls=%async_computation.5 | async-start | bytes 4194304 | tf_op jit(solution)/shard_map/all_to_all | solution.py:119
  1269.4 29.1 %all-to-all-start.6 = ((bf16[4096,2,128]{2,1,0:T(2,128)(2,1)}), bf16[4096,2,128]{2,1,0:T(2,128)(2,1)S(1)}, u32[]{:S(2)}, u32[]{:S(2)}) async-start(bf16[4096,2,128]{2,1,0:T(2,128)(2,1)} %copy.99), calls=%async_computation.6 | async-start | bytes 4194304 | tf_op jit(solution)/shard_map/all_to_all | solution.py:119
  1272.0 282.2 %reduce-scatter.8.cloned.1.call-start = ((), (), s32[]{:S(2)}) async-start(), calls=%async_computation.22 | async-start | bytes 18874368 | tf_op jit(solution)/shard_map/reduce_scatter | solution.py:113
  1321.7 236.6 %reduce-scatter.10.cloned.1.call-start = ((), (), s32[]{:S(2)}) async-start(), calls=%async_computation.23 | async-start | bytes 18874368 | tf_op jit(solution)/shard_map/reduce_scatter | solution.py:113
  1331.4 331.6 %reduce-scatter.12.cloned.1.call-start = ((), (), s32[]{:S(2)}) async-start(), calls=%async_computation.24 | async-start | bytes 18874368 | tf_op jit(solution)/shard_map/reduce_scatter | solution.py:113
  1390.3 383.8 %reduce-scatter.14.cloned.1.call-start = ((), (), s32[]{:S(2)}) async-start(), calls=%async_computation.25 | async-start | bytes 18874368 | tf_op jit(solution)/shard_map/reduce_scatter | solution.py:113
  1401.7 626.1 %reduce-scatter.16.cloned.1.call-start = ((), (), s32[]{:S(2)}) async-start(), calls=%async_computation.26 | async-start | bytes 50724864 | tf_op jit(solution)/shard_map/reduce_scatter | solution.py:113
  1425.9 855.8 %reduce-scatter.18.cloned.1.call-start = ((), (), s32[]{:S(2)}) async-start(), calls=%async_computation.27 | async-start | bytes 50724864 | tf_op jit(solution)/shard_map/reduce_scatter | solution.py:113
  1451.2 1084.1 %reduce-scatter.20.cloned.1.call-start = ((), (), s32[]{:S(2)}) async-start(), calls=%async_computation.28 | async-start | bytes 50724864 | tf_op jit(solution)/shard_map/reduce_scatter | solution.py:113
  1475.0 19.5 copy-start.34
  1494.5 9.6 copy-start.33
  1504.1 9.9 copy-start.14
  1504.1 9.9 copy-start.31
  1513.9 10.9 copy-start.44
  (126 other events, 521.6 us)
Sparse Core Ops, SparseCore 0:
  10.4 52.9 all-gather.12
  65.8 49.9 all-gather.10
  118.2 78.0 all-gather.14
  197.9 72.7 all-gather.16
  272.4 108.5 all-gather.18
  382.6 131.1 all-gather.22
  515.6 108.4 all-gather.20
  1321.8 118.9 reduce-scatter.7
  1444.4 108.3 reduce-scatter.9
  1556.1 106.9 reduce-scatter.11
  1667.1 106.9 reduce-scatter.13
  1778.2 249.5 reduce-scatter.15
  2032.0 249.5 reduce-scatter.17
  2285.7 249.5 reduce-scatter.19
where the time goes:
time: 2550 us; the launch traced here: 2540 us
  waiting for transfers between devices  1220 us (48%)
  matrix products  691 us (27%)
  blocking collectives  210 us (8%)
  other arithmetic  182 us (7%)
  local copies, waits for them, and re-layouts  178 us (7%)
    reduce_scatter x7, waiting for transfers between devices, scatter_sum(): return lax.psum_scatter(t, 'sp', scatter_dimension=0, tiled=True)  969 us
    all_gather x7, waiting for transfers between devices, gather(): return lax.all_gather(t, 'sp', axis=0, tiled=True)  191 us
    dot_general x16, matrix products, step(): jnp.einsum('grqk,qgrd->kgd', grad_s, q_block, preferred_element_type=jnp....  105 us
    all_gather x3, blocking collectives, gather(): return lax.all_gather(t, 'sp', axis=0, tiled=True)  105 us
    dot_general x32, matrix products, block_probs(): jnp.einsum('qgrd,kgd->grqk', q_block, k_all, preferred_element_type=jnp.f...  94.5 us
    another operation x16, other arithmetic  77.6 us
    while x224, local copies, waits for them, and re-layouts  66.1 us
    dot_general x16, matrix products, step(): jnp.einsum('qgrd,kgd->grqk', go_block, v_all, preferred_element_type=jnp....  56.9 us
  transfers between devices with their start and end apart: 20, of which 13 were waited for; matrix products, arithmetic and copies ran while one was open for 17% of the time, Pallas kernels for 0%

commit v1 on v0

v1 whole, which is shorter than its diff:
```python
import functools

import jax
import jax.numpy as jnp
from jax import lax
from jax.experimental import pallas as pl
from jax.experimental.pallas import tpu as pltpu
from jax.sharding import PartitionSpec as P

NORM_EPS = 1e-5
ROPE_BASE = 10000.0
BF = jnp.bfloat16
F32 = jnp.float32
BQ = 256
BK = 512
NEG = -1e30


def dot(a, b):
    return lax.dot_general(a, b, (((1,), (0,)), ((), ())), preferred_element_type=F32)


def dot_nt(a, b):
    return lax.dot_general(a, b, (((1,), (1,)), ((), ())), preferred_element_type=F32)


def dot_tn(a, b):
    return lax.dot_general(a, b, (((0,), (0,)), ((), ())), preferred_element_type=F32)


def allowed_block(i, j, start_row):
    kv = j * BK + lax.broadcasted_iota(jnp.int32, (BK, BQ), 0)
    qi = i * BQ + lax.broadcasted_iota(jnp.int32, (BK, BQ), 1)
    return (kv <= qi) & (kv >= start_row)


def attn_fwd_kernel(scale, lo_ref, q_ref, k_ref, vt_ref, start_ref, o_ref, lse_ref, s_scr):
    i = pl.program_id(1)
    lo = lo_ref[i]
    hi = (i * BQ + BQ - 1) // BK + 1
    q = q_ref[...]
    start_row = start_ref[0]

    def first(j, carry):
        m, l = carry
        kb = k_ref[pl.ds(pl.multiple_of(j * BK, BK), BK), :]
        s = dot_nt(kb, q) * scale
        s = jnp.where(allowed_block(i, j, start_row), s, NEG)
        s_scr[j] = s
        m_new = jnp.maximum(m, jnp.max(s, axis=0, keepdims=True))
        l = l * jnp.exp(m - m_new) + jnp.sum(jnp.exp(s - m_new), axis=0, keepdims=True)
        return m_new, l

    m, l = lax.fori_loop(lo, hi, first, (jnp.full((1, BQ), NEG, F32), jnp.zeros((1, BQ), F32)))
    lse = m + jnp.log(l)
    lse_ref[0, 0] = lse

    def second(j, acc):
        p = jnp.exp(s_scr[j] - lse).astype(BF)
        return acc + dot(vt_ref[:, pl.ds(pl.multiple_of(j * BK, BK), BK)], p)

    acc = lax.fori_loop(lo, hi, second, jnp.zeros((q.shape[1], BQ), F32))
    o_ref[...] = acc.T.astype(BF)


def attn_forward(q, k, vt, starts):
    tokens, width = q.shape
    hd = 128
    heads = width // hd
    nq = tokens // BQ
    lo = starts[::BQ] // BK
    grid_spec = pltpu.PrefetchScalarGridSpec(
        num_scalar_prefetch=1, grid=(heads, nq),
        in_specs=[pl.BlockSpec((BQ, hd), lambda h, i, *_: (i, h)),
                  pl.BlockSpec((tokens, hd), lambda h, i, *_: (0, h)),
                  pl.BlockSpec((hd, tokens), lambda h, i, *_: (h, 0)),
                  pl.BlockSpec((1, 1, BQ), lambda h, i, *_: (i, 0, 0))],
        out_specs=[pl.BlockSpec((BQ, hd), lambda h, i, *_: (i, h)),
                   pl.BlockSpec((1, 1, 1, BQ), lambda h, i, *_: (h, i, 0, 0))],
        scratch_shapes=[pltpu.VMEM((tokens // BK, BK, BQ), F32)])
    return pl.pallas_call(
        functools.partial(attn_fwd_kernel, hd ** -0.5),
        grid_spec=grid_spec,
        out_shape=[jax.ShapeDtypeStruct((tokens, width), BF),
                   jax.ShapeDtypeStruct((heads, nq, 1, BQ), F32)],
        compiler_params=pltpu.CompilerParams(dimension_semantics=("arbitrary", "arbitrary"),
                                             vmem_limit_bytes=40 * 1024 * 1024),
        cost_estimate=pl.CostEstimate(flops=25_000_000_000, bytes_accessed=10_000_000, transcendentals=10_000_000),
        name="attn_fwd",
    )(lo, q, k, vt, starts.reshape(nq, 1, BQ))


def attn_bwd_kernel(scale, lo_ref, q_ref, do_ref, k_ref, v_ref, kt_ref, lse_ref, delta_ref, start_ref,
                    dq_ref, dk_ref, dv_ref, dk_acc, dv_acc):
    i = pl.program_id(1)
    lo = lo_ref[i]
    hi = (i * BQ + BQ - 1) // BK + 1

    @pl.when(i == 0)
    def _():
        dk_acc[...] = jnp.zeros_like(dk_acc)
        dv_acc[...] = jnp.zeros_like(dv_acc)

    q = q_ref[...]
    do = do_ref[...]
    start_row = start_ref[0]
    lse = lse_ref[0, 0]
    delta = delta_ref[0, 0]

    def body(j, dqt):
        rows = pl.ds(pl.multiple_of(j * BK, BK), BK)
        s = dot_nt(k_ref[rows, :], q) * scale
        p = jnp.where(allowed_block(i, j, start_row), jnp.exp(s - lse), 0.0)
        dv_acc[rows, :] += dot(p.astype(BF), do)
        dp = dot_nt(v_ref[rows, :], do).astype(BF).astype(F32)
        ds = (p * (dp - delta) * scale).astype(BF)
        dk_acc[rows, :] += dot(ds, q)
        return dqt + dot(kt_ref[:, rows], ds)

    dqt = lax.fori_loop(lo, hi, body, jnp.zeros((q.shape[1], BQ), F32))
    dq_ref[...] = dqt.T.astype(BF)

    @pl.when(i == pl.num_programs(1) - 1)
    def _():
        dk_ref[...] = dk_acc[...].astype(BF)
        dv_ref[...] = dv_acc[...].astype(BF)


def attn_backward(q, k, v, kt, grad_o, lse, delta, starts):
    tokens, width = q.shape
    hd = 128
    heads = width // hd
    nq = tokens // BQ
    lo = starts[::BQ] // BK
    row = pl.BlockSpec((BQ, hd), lambda h, i, *_: (i, h))
    col = pl.BlockSpec((tokens, hd), lambda h, i, *_: (0, h))
    stat = pl.BlockSpec((1, 1, 1, BQ), lambda h, i, *_: (h, i, 0, 0))
    grid_spec = pltpu.PrefetchScalarGridSpec(
        num_scalar_prefetch=1, grid=(heads, nq),
        in_specs=[row, row, col, col,
                  pl.BlockSpec((hd, tokens), lambda h, i, *_: (h, 0)),
                  stat, stat,
                  pl.BlockSpec((1, 1, BQ), lambda h, i, *_: (i, 0, 0))],
        out_specs=[row, col, col],
        scratch_shapes=[pltpu.VMEM((tokens, hd), F32), pltpu.VMEM((tokens, hd), F32)])
    out = jax.ShapeDtypeStruct((tokens, width), BF)
    return pl.pallas_call(
        functools.partial(attn_bwd_kernel, hd ** -0.5),
        grid_spec=grid_spec,
        out_shape=[out, out, out],
        compiler_params=pltpu.CompilerParams(dimension_semantics=("arbitrary", "arbitrary"),
                                             vmem_limit_bytes=40 * 1024 * 1024),
        cost_estimate=pl.CostEstimate(flops=60_000_000_000, bytes_accessed=20_000_000, transcendentals=10_000_000),
        name="attn_bwd",
    )(lo, q, grad_o, k, v, kt, lse, delta, starts.reshape(nq, 1, BQ))


def rms_back(grad_out, normed, inv_rms):
    mean_term = jnp.mean(grad_out * normed, axis=-1, keepdims=True)
    return inv_rms * (grad_out - normed * mean_term)


def solution(mesh):
    row_spec = P('sp', None)
    cube_spec = P('sp', None, None)
    vec_spec = P('sp')
    n = mesh.shape['sp']

    def gather(t):
        return lax.all_gather(t, 'sp', axis=0, tiled=True)

    def swap(t, mask):
        return lax.ppermute(t, 'sp', [(d, d ^ mask) for d in range(n)])

    def pick(t, index, axis=0):
        return lax.dynamic_index_in_dim(t, index, axis, keepdims=False)

    def halves(mine, other, pos):
        first = jnp.where(pos == 0, mine, other)
        second = jnp.where(pos == 0, other, mine)
        return jnp.concatenate([first, second], axis=0)

    def local_layer(x, seg_ids, positions, grad_y, norm1_gain, w_q, w_k, w_v, w_o, norm2_gain, w_gate, w_up, w_down):
        tl, d = x.shape
        tokens = tl * n
        dr = w_gate.shape[0]
        ff = w_gate.shape[1]
        fr = w_down.shape[0]
        hw = d // n
        head_dim = w_q.shape[2]
        me = lax.axis_index('sp')
        yy = me // 4
        qq = me % 4
        xx = qq // 2
        cc = qq % 2

        small = gather(jnp.concatenate([norm1_gain.astype(F32), norm2_gain.astype(F32),
                                        positions.astype(F32)])[None])
        gain1 = small[:, :dr].reshape(-1)
        gain2 = small[:, dr:2 * dr].reshape(-1)
        pos_all = small[:, 2 * dr:].reshape(-1)
        starts = jnp.arange(tokens, dtype=jnp.int32) - pos_all.astype(jnp.int32)

        half = head_dim // 2
        inv_freq = ROPE_BASE ** (-jnp.arange(half, dtype=F32) * 2.0 / head_dim)
        angle = pos_all[:, None] * inv_freq[None, :]
        cos_t, sin_t = jnp.cos(angle), jnp.sin(angle)
        cos_full = jnp.concatenate([cos_t] * 4, axis=-1)
        sin_full = jnp.concatenate([sin_t] * 4, axis=-1)

        def rotate_half(t):
            parts = []
            for h in range(t.shape[-1] // head_dim):
                lo = t[:, h * head_dim:h * head_dim + half]
                hi = t[:, h * head_dim + half:(h + 1) * head_dim]
                parts += [-hi, lo]
            return jnp.concatenate(parts, axis=-1)

        def rope_apply(t):
            return t * cos_full + rotate_half(t) * sin_full

        def rope_back(t):
            return t * cos_full - rotate_half(t) * sin_full

        x_wide = x.astype(F32)
        inv_rms1 = lax.rsqrt(jnp.mean(x_wide * x_wide, axis=-1, keepdims=True) + NORM_EPS)
        normed1 = x_wide * inv_rms1
        u_norm = (normed1 * gain1).astype(BF)
        u_all = gather(u_norm)

        def quarter_rows(w4):
            blocks = [pick(w4, qq)] + [swap(pick(w4, qq ^ m), m) for m in (1, 2, 3)]
            out = jnp.zeros((4,) + w4.shape[1:], w4.dtype)
            for m in range(4):
                out = lax.dynamic_update_slice(out, blocks[m][None], (qq ^ m, 0, 0))
            return out.reshape(4 * dr, -1)

        wqkv = jnp.stack([w.reshape(dr, 2, 4, hw) for w in (w_q, w_k, w_v)], axis=1)
        wqkv = wqkv.transpose(3, 0, 2, 1, 4).reshape(4, dr, 6 * hw)
        s_qkv = quarter_rows(wqkv)
        s_own = lax.dynamic_slice_in_dim(s_qkv, yy * 3 * hw, 3 * hw, 1)
        s_oth = lax.dynamic_slice_in_dim(s_qkv, (1 - yy) * 3 * hw, 3 * hw, 1)
        w_own = halves(s_own, swap(s_oth, 4), yy)

        qkv = dot(u_all, w_own)
        q = rope_apply(qkv[:, :hw]).astype(BF)
        k = rope_apply(qkv[:, hw:2 * hw]).astype(BF)
        v = qkv[:, 2 * hw:].astype(BF)
        o, lse = attn_forward(q, k, v.T, starts)

        o_loc = lax.all_to_all(o, 'sp', 0, 1, tiled=True)
        wo_own = w_o.reshape(hw, d)
        wo_full = gather(wo_own)
        gy_all = gather(grad_y)

        def ff_quarter(w):
            w4 = w.reshape(dr, 2, 4, fr).transpose(2, 0, 1, 3).reshape(4, dr, 2 * fr)
            mine = quarter_rows(w4)
            return halves(mine, swap(mine, 4), yy)

        wd_quarter = halves(w_down, swap(w_down, 4), yy)
        wg_quarter = ff_quarter(w_gate)
        wu_quarter = ff_quarter(w_up)

        h_res = (x_wide + dot(o_loc, wo_full)).astype(BF)
        h_wide = h_res.astype(F32)
        inv_rms2 = lax.rsqrt(jnp.mean(h_wide * h_wide, axis=-1, keepdims=True) + NORM_EPS)
        normed2 = h_wide * inv_rms2
        z_norm = (normed2 * gain2).astype(BF)
        z_all = gather(z_norm)

        grad_act = dot_nt(gy_all, wd_quarter).astype(BF).astype(F32)
        gate_pre = dot(z_all, wg_quarter)
        up_pre = dot(z_all, wu_quarter)
        gate_sig = jax.nn.sigmoid(gate_pre)
        gate_act = gate_pre * gate_sig
        mlp_act = (gate_act * up_pre).astype(BF)
        grad_gate = (grad_act * up_pre * gate_sig * (1.0 + gate_pre * (1.0 - gate_sig))).astype(BF)
        grad_up = (grad_act * gate_act).astype(BF)

        def token_half(t):
            return lax.dynamic_slice_in_dim(t, yy * 4 * tl, 4 * tl, 0)

        def quarter_sum(part):
            part = part.reshape(2, 2, tl, d)
            kept = pick(part, cc, 1) + swap(pick(part, 1 - cc, 1), 1)
            return pick(kept, xx) + swap(pick(kept, 1 - xx), 2)

        gz = quarter_sum(dot_nt(token_half(grad_gate), wg_quarter) + dot_nt(token_half(grad_up), wu_quarter))
        gz = gz.astype(BF).astype(F32)
        grad_gain2 = jnp.sum(gz * normed2, axis=0)
        grad_h = (grad_y.astype(F32) + rms_back(gz * gain2, normed2, inv_rms2)).astype(BF)
        gh_all = gather(grad_h)

        y = (h_wide + quarter_sum(dot(token_half(mlp_act), wd_quarter))).astype(BF)

        z_cols = lax.dynamic_slice_in_dim(z_all, yy * 4 * dr, 4 * dr, 1)

        def spread_rows(g):
            g4 = g.reshape(4, dr, 2 * fr)
            blocks = [pick(g4, qq)] + [swap(pick(g4, qq ^ m), m) for m in (1, 2, 3)]
            out = jnp.zeros((4, dr, 2 * fr), F32)
            for m in range(4):
                out = lax.dynamic_update_slice(out, blocks[m][None], (qq ^ m, 0, 0))
            return out.reshape(4, dr, 2, fr).transpose(1, 2, 0, 3).reshape(dr, ff)

        grad_wgate = spread_rows(dot_tn(z_cols, grad_gate))
        grad_wup = spread_rows(dot_tn(z_cols, grad_up))
        grad_wdown = dot_tn(lax.dynamic_slice_in_dim(mlp_act, yy * fr, fr, 1), gy_all)

        grad_o = dot_nt(gh_all, wo_own).astype(BF)
        grad_wo = dot_tn(o, gh_all)
        delta = jnp.sum((grad_o.astype(F32) * o.astype(F32)).reshape(tokens, -1, head_dim), axis=-1)
        delta = delta.T.reshape(lse.shape)
        dq, dk, dv = attn_backward(q, k, v, k.T, grad_o, lse, delta, starts)
        dq_pre = rope_back(dq.astype(F32)).astype(BF)
        dk_pre = rope_back(dk.astype(F32)).astype(BF)
        dqkv = jnp.concatenate([dq_pre, dk_pre, dv], axis=1)

        d_own = token_half(dqkv)
        d_oth = swap(lax.dynamic_slice_in_dim(dqkv, (1 - yy) * 4 * tl, 4 * tl, 0), 4)
        w_oth = halves(s_oth, swap(s_own, 4), yy)
        gu = quarter_sum(dot_nt(d_own, w_own) + dot_nt(d_oth, w_oth))
        gu = gu.astype(BF).astype(F32)

        def spread_heads(g):
            return lax.all_to_all(g, 'sp', 0, 1, tiled=True)

        grad_wq = spread_heads(dot_tn(u_all, dq_pre))
        grad_wk = spread_heads(dot_tn(u_all, dk_pre))
        grad_wv = spread_heads(dot_tn(u_all, dv))

        grad_gain1 = jnp.sum(gu * normed1, axis=0)
        grad_x = (grad_h.astype(F32) + rms_back(gu * gain1, normed1, inv_rms1)).astype(BF)
        gains = jnp.stack([grad_gain1.reshape(n, dr), grad_gain2.reshape(n, dr)], axis=1)
        gains = jnp.sum(lax.all_to_all(gains, 'sp', 0, 0, tiled=True), axis=0)
        return (y, grad_x, gains[0], grad_wq.reshape(w_q.shape), grad_wk.reshape(w_k.shape),
                grad_wv.reshape(w_v.shape), grad_wo.reshape(w_o.shape), gains[1], grad_wgate, grad_wup, grad_wdown)

    return jax.shard_map(
        local_layer, mesh=mesh,
        in_specs=(row_spec, vec_spec, vec_spec, row_spec, vec_spec, cube_spec, cube_spec, cube_spec, cube_spec,
                  vec_spec, row_spec, row_spec, row_spec),
        out_specs=(row_spec, row_spec, vec_spec, cube_spec, cube_spec, cube_spec, cube_spec, vec_spec,
                   row_spec, row_spec, row_spec),
        check_vma=False)
```

time: 2550 us -> 1680 us (0.66)
  waiting for transfers between devices: 1220 us -> 750 us
  matrix products: 691 us -> 325 us
  blocking collectives: 210 us -> 13.8 us
  Pallas kernels: 0 us -> 110 us
  local copies, waits for them, and re-layouts: 178 us -> 281 us
  other arithmetic: 182 us -> 136 us
    reduce_scatter x7 -> x0, waiting for transfers between devices: 969 us -> none  [scatter_sum(): return lax.psum_scatter(t, 'sp', scatter_dimension=0, tiled=True)]
    ppermute x0 -> x27, waiting for transfers between devices: none -> 538 us  [swap(): return lax.ppermute(t, 'sp', [(d, d ^ mask) for d in range(n)])]
    dot_general x131 -> x18, matrix products: 677 us -> 325 us  [the longest x5 120 us: dot(): lax.dot_general(a, b, (((1,), (0,)), ((), ())), preferred_element_type=F32)]
    all_gather x7 -> x5, waiting for transfers between devices: 191 us -> 62.1 us  [gather(): return lax.all_gather(t, 'sp', axis=0, tiled=True)]
    pallas_call x0 -> x2, Pallas kernels: none -> 110 us  [the longest x1 56.7 us: attn_backward(): pl.pallas_call(functools.partial(attn_bwd_kernel, hd ** (-0.5)), grid_spe...]
    all_gather x3 -> x1, blocking collectives: 105 us -> 13.8 us  [gather(): return lax.all_gather(t, 'sp', axis=0, tiled=True)]
    all_to_all x6 -> x5, waiting for transfers between devices: 58 us -> 148 us  [the longest x3 122 us: spread_heads(): return lax.all_to_all(g, 'sp', 0, 1, tiled=True)]
    while x227 -> x0, local copies, waits for them, and re-layouts: 82.9 us -> none
  transfers between devices with their start and end apart: 20 -> 37, of which waited for: 13 -> 18; matrix products, arithmetic and copies ran while one was open for 17% -> 31% of each run, Pallas kernels for 0% -> 3%
where the time goes in v1:
time: 1680 us; the launch traced here: 1660 us
  waiting for transfers between devices  750 us (45%)
  matrix products  325 us (19%)
  local copies, waits for them, and re-layouts  281 us (17%)
  other arithmetic  136 us (8%)
  Pallas kernels  110 us (7%)
  starting transfers between devices  33.6 us (2%)
    ppermute x27, waiting for transfers between devices, swap(): return lax.ppermute(t, 'sp', [(d, d ^ mask) for d in range(n)])  538 us
    all_to_all x3, waiting for transfers between devices, spread_heads(): return lax.all_to_all(g, 'sp', 0, 1, tiled=True)  122 us
    dot_general x5, matrix products, dot(): lax.dot_general(a, b, (((1,), (0,)), ((), ())), preferred_element_type=F32)  120 us
    dot_general x6, matrix products, dot_nt(): lax.dot_general(a, b, (((1,), (1,)), ((), ())), preferred_element_type=F32)  113 us
    dot_general x7, matrix products, dot_tn(): lax.dot_general(a, b, (((0,), (0,)), ((), ())), preferred_element_type=F32)  90.9 us
    all_gather x5, waiting for transfers between devices, gather(): return lax.all_gather(t, 'sp', axis=0, tiled=True)  62.1 us
    pallas_call x1, Pallas kernels, attn_backward(): pl.pallas_call(functools.partial(attn_bwd_kernel, hd ** (-0.5)), grid_spe...  56.7 us
    unnamed x172, local copies, waits for them, and re-layouts  55.1 us
  transfers between devices with their start and end apart: 37, of which 18 were waited for; matrix products, arithmetic and copies ran while one was open for 31% of the time, Pallas kernels for 3%

profile of v1, /device:TPU:0, one launch (start us, length us, event | category | flops | bytes accessed | tf_op | source)
XLA Modules:
  0.0 1662.8 jit_solution(9733600367347789893)
XLA Ops:
  9.2 13.8 all-gather
  49.0 28.9 %collective-permute-done.1 = bf16[256,1536]{1,0:T(8,128)(2,1)} collective-permute-done((bf16[256,1536]{1,0:T(8,128)(2,1)}, bf16[256,1536]{1,0:T(8,128)(2,1)}, u32[]{:S(2)}, u32[]{:S(2)}) %collective-permute-start.1) | collective-permute-done | bytes 786464 | tf_op jit(solution)/shard_map/ppermute | solution.py:173
  79.1 25.9 %collective-permute-done.2 = bf16[256,1536]{1,0:T(8,128)(2,1)} collective-permute-done((bf16[256,1536]{1,0:T(8,128)(2,1)}, bf16[256,1536]{1,0:T(8,128)(2,1)}, u32[]{:S(2)}, u32[]{:S(2)}) %collective-permute-start.2) | collective-permute-done | bytes 786464 | tf_op jit(solution)/shard_map/ppermute | solution.py:173
  109.1 55.3 %collective-permute-done.18 = bf16[1024,768]{1,0:T(8,128)(2,1)} collective-permute-done((bf16[1024,768]{1,0:T(8,128)(2,1)}, bf16[1024,768]{1,0:T(8,128)(2,1)}, u32[]{:S(2)}, u32[]{:S(2)}) %collective-permute-start.18) | collective-permute-done | bytes 1572896 | tf_op jit(solution)/shard_map/ppermute | solution.py:173
  172.3 57.8 %collective-permute-done.3 = bf16[1024,768]{1,0:T(8,128)(2,1)} collective-permute-done((bf16[1024,768]{1,0:T(8,128)(2,1)}, bf16[1024,768]{1,0:T(8,128)(2,1)}, u32[]{:S(2)}, u32[]{:S(2)}) %collective-permute-start.3) | collective-permute-done | bytes 1572896 | tf_op jit(solution)/shard_map/ppermute | solution.py:173
  234.2 20.6 %fusion.59 = f32[4096,768]{0,1:T(8,128)} fusion(bf16[4096,2048]{1,0:T(8,128)(2,1)} %all-gather.7.cloned.1.call-done, bf16[1024,768]{1,0:T(8,128)(2,1)} %get-tuple-element.125, bf16[1024,768]{1,0:T(8,128)(2,1)} %get-tuple-element.124), kind=kOutput, calls=%fused_computation.108 | convolution fusion | flops 12891193344 | bytes 32505856 | tf_op jit(solution)/shard_map/dot_general | solution.py:20
  293.4 52.8 %attn_fwd.1 = (bf16[4096,256]{1,0:T(8,128)(2,1)S(1)}, f32[2,16,1,256]{3,2,1,0:T(1,128)S(1)}) custom-call(s32[16]{0:T(128)S(1)} %and_select_fusion.lo_ref, bf16[4096,256]{1,0:T(8,128)(2,1)S(1)} %copy-done.5, bf16[4096,256]{1,0:T(8,128)(2,1)S(1)} %copy-done.3, bf16[256,4096]{1,0:T(8,128)(2,1)S(1)} %copy-done.13, s32[16,1,256]{2,1,0:T(1,128)S(1)} %add_subtract_fusion.start_ref), custom_call_target="tpu_custom_call" | custom-call | flops 24999999488 | bytes 10000000 | tf_op jit(solution)/shard_map/attn_fwd/pallas_call | solution.py:81
  352.3 26.2 %all-to-all-done = bf16[8,512,256]{1,2,0:T(8,128)(2,1)} async-done(((bf16[8,512,256]{1,2,0:T(8,128)(2,1)}), bf16[8,512,256]{1,2,0:T(8,128)(2,1)}, u32[]{:S(2)}, u32[]{:S(2)}) %all-to-all-start) | async-done | bytes 2097184 | tf_op jit(solution)/shard_map/all_to_all | solution.py:251
  378.5 9.6 fusion.40
  411.7 18.9 %collective-permute-done.5 = bf16[256,1376]{0,1:T(8,128)(2,1)} collective-permute-done((bf16[256,1376]{0,1:T(8,128)(2,1)}, bf16[256,1376]{0,1:T(8,128)(2,1)}, u32[]{:S(2)}, u32[]{:S(2)}) %collective-permute-start.5) | collective-permute-done | bytes 704544 | tf_op jit(solution)/shard_map/ppermute | solution.py:173
  433.0 21.4 %collective-permute-done.6 = bf16[256,1376]{0,1:T(8,128)(2,1)} collective-permute-done((bf16[256,1376]{0,1:T(8,128)(2,1)}, bf16[256,1376]{0,1:T(8,128)(2,1)}, u32[]{:S(2)}, u32[]{:S(2)}) %collective-permute-start.6) | collective-permute-done | bytes 704544 | tf_op jit(solution)/shard_map/ppermute | solution.py:173
  469.4 15.9 collective-permute-done.9
  487.5 27.2 %collective-permute-done.10 = bf16[256,1376]{0,1:T(8,128)(2,1)} collective-permute-done((bf16[256,1376]{0,1:T(8,128)(2,1)}, bf16[256,1376]{0,1:T(8,128)(2,1)}, u32[]{:S(2)}, u32[]{:S(2)}) %collective-permute-start.10) | collective-permute-done | bytes 704544 | tf_op jit(solution)/shard_map/ppermute | solution.py:173
  523.3 15.9 collective-permute-done.12
  544.8 55.1 %collective-permute-done.7 = bf16[1024,1376]{0,1:T(8,128)(2,1)} collective-permute-done((bf16[1024,1376]{0,1:T(8,128)(2,1)}, bf16[1024,1376]{0,1:T(8,128)(2,1)}, u32[]{:S(2)}, u32[]{:S(2)}) %collective-permute-start.7) | collective-permute-done | bytes 2818080 | tf_op jit(solution)/shard_map/ppermute | solution.py:173
  604.4 54.3 %collective-permute-done.11 = bf16[1024,1376]{0,1:T(8,128)(2,1)} collective-permute-done((bf16[1024,1376]{0,1:T(8,128)(2,1)}, bf16[1024,1376]{0,1:T(8,128)(2,1)}, u32[]{:S(2)}, u32[]{:S(2)}) %collective-permute-start.11) | collective-permute-done | bytes 2818080 | tf_op jit(solution)/shard_map/ppermute | solution.py:173
  672.4 30.3 %convolution_convert_fusion = bf16[1376,4096]{1,0:T(8,128)(2,1)} fusion(bf16[4096,2048]{1,0:T(8,128)(2,1)} %all-gather.13.cloned.1.call-done, bf16[688,2048]{1,0:T(8,128)(2,1)} %get-tuple-element.119, bf16[688,2048]{1,0:T(8,128)(2,1)} %get-tuple-element.118), kind=kOutput, calls=%fused_computation.9 | convolution fusion | flops 23102357504 | bytes 33685504 | tf_op jit(solution)/shard_map/dot_general | solution.py:24
  702.7 29.9 %fusion.53 = f32[4096,1376]{0,1:T(8,128)} fusion(bf16[4096,2048]{1,0:T(8,128)(2,1)} %all-gather.11.cloned.1.call-done, bf16[1024,1376]{1,0:T(8,128)(2,1)} %get-tuple-element.107, bf16[1024,1376]{1,0:T(8,128)(2,1)S(1)} %copy-done.53), kind=kOutput, calls=%fused_computation.94 | convolution fusion | flops 23096721408 | bytes 44957696 | tf_op jit(solution)/shard_map/dot_general | solution.py:20
  732.6 42.2 %fusion.2 = (bf16[4096,1376]{0,1:T(8,128)(2,1)}, bf16[4096,1376]{0,1:T(8,128)(2,1)}, bf16[4096,1376]{0,1:T(8,128)(2,1)}) fusion(bf16[1376,4096]{1,0:T(8,128)(2,1)} %convolution_convert_fusion, f32[4096,1376]{0,1:T(8,128)} %fusion.53, bf16[4096,2048]{1,0:T(8,128)(2,1)} %all-gather.11.cloned.1.call-done, bf16[1024,1376]{1,0:T(8,128)(2,1)} %get-tuple-element.109, ...), kind=kOutput, calls=%fused_computation.4 | convolution fusion | flops 23186898944 | bytes 90046464 | tf_op jit(solution)/shard_map/dot_general | solution.py:20
  774.8 19.7 %fusion.19 = f32[2048,2048]{1,0:T(8,128)} fusion(bf16[4096,1376]{0,1:T(8,128)(2,1)} %get-tuple-element.97, s32[]{:T(128)S(6)} %select_n.187, bf16[1024,1376]{1,0:T(8,128)(2,1)} %get-tuple-element.109, bf16[1024,1376]{1,0:T(8,128)(2,1)S(1)} %copy-done.54), kind=kOutput, calls=%fused_computation.42 | convolution fusion | flops 11553996800 | bytes 28114948 | tf_op jit(solution)/shard_map/dot_general | solution.py:24
  794.5 22.0 %convolution_add_fusion = f32[2048,2048]{1,0:T(8,128)} fusion(f32[2048,2048]{1,0:T(8,128)} %fusion.19, bf16[4096,1376]{0,1:T(8,128)(2,1)} %get-tuple-element.95, s32[]{:T(128)S(6)} %select_n.187, bf16[1024,1376]{1,0:T(8,128)(2,1)} %get-tuple-element.107, bf16[1024,1376]{1,0:T(8,128)(2,1)S(1)} %copy-done.53), kind=kOutput, calls=%fused_computation.16 | convolution fusion | flops 11558191104 | bytes 44892164 | tf_op jit(solution)/shard_map/dot_general | solution.py:24
  816.5 7.8 dynamic-slice_bitcast_fusion.1
  824.4 18.1 %fusion.22 = f32[2048,2048]{1,0:T(8,128)} fusion(bf16[4096,1376]{0,1:T(8,128)(2,1)} %get-tuple-element.96, s32[]{:T(128)S(6)} %select_n.187, bf16[688,2048]{1,0:T(8,128)(2,1)S(1)} %copy-done.56, bf16[688,2048]{1,0:T(8,128)(2,1)S(1)} %copy-done.55), kind=kOutput, calls=%fused_computation.45 | convolution fusion | flops 11553996800 | bytes 28049412 | tf_op jit(solution)/shard_map/dot_general | solution.py:20
  842.5 7.7 dynamic-slice_bitcast_fusion.2
  850.7 11.7 bitcast_add_fusion.1
  867.6 11.7 bitcast_add_fusion.2
  885.7 74.9 %collective-permute-done.16 = f32[512,2048]{1,0:T(8,128)} collective-permute-done((f32[512,2048]{1,0:T(8,128)}, f32[512,2048]{1,0:T(8,128)}, u32[]{:S(2)}, u32[]{:S(2)}) %collective-permute-start.16) | collective-permute-done | bytes 4194336 | tf_op jit(solution)/shard_map/ppermute | solution.py:173
  966.0 83.5 %collective-permute-done.14 = f32[512,2048]{1,0:T(8,128)} collective-permute-done((f32[512,2048]{1,0:T(8,128)}, f32[512,2048]{1,0:T(8,128)}, u32[]{:S(2)}, u32[]{:S(2)}) %collective-permute-start.14) | collective-permute-done | bytes 4194336 | tf_op jit(solution)/shard_map/ppermute | solution.py:173
  1057.7 18.3 %fusion.5 = f32[1024,1376]{0,1:T(8,128)} fusion(bf16[4096,1376]{0,1:T(8,128)(2,1)} %get-tuple-element.95, bf16[4096,2048]{1,0:T(8,128)(2,1)} %all-gather.11.cloned.1.call-done, s32[]{:T(128)S(6)} %select_n.200), kind=kOutput, calls=%fused_computation.17 | convolution fusion | flops 11542724608 | bytes 25296900 | tf_op jit(solution)/shard_map/dot_general | solution.py:28
  1076.1 62.0 %all-gather.15.cloned.1.call-done = bf16[4096,2048]{1,0:T(8,128)(2,1)} async-done(((bf16[512,2048]{1,0:T(8,128)(2,1)}), bf16[4096,2048]{1,0:T(8,128)(2,1)}) %all-gather.15.cloned.1.call-update) | async-done | bytes 16777232 | tf_op jit(solution)/shard_map/all_gather | solution.py:170
  1138.1 13.3 convert_multiply_fusion.6
  1157.1 9.6 reduce_sum.75
  1172.1 56.7 %attn_bwd.1 = (bf16[4096,256]{1,0:T(8,128)(2,1)S(1)}, bf16[4096,256]{1,0:T(8,128)(2,1)S(1)}, bf16[4096,256]{1,0:T(8,128)(2,1)S(1)}) custom-call(s32[16]{0:T(128)S(1)} %copy-done.17, bf16[4096,256]{1,0:T(8,128)(2,1)S(1)} %copy-done.6, bf16[4096,256]{1,0:T(8,128)(2,1)S(1)} %copy-done.18, bf16[4096,256]{1,0:T(8,128)(2,1)S(1)} %copy-done.4, ...), custom_call_target="tpu_custom_call" | custom-call | flops 60000002048 | bytes 20000000 | tf_op jit(solution)/shard_map/attn_bwd/pallas_call | solution.py:147
  1266.6 18.1 %fusion.7 = f32[1024,1376]{0,1:T(8,128)} fusion(bf16[4096,1376]{0,1:T(8,128)(2,1)} %get-tuple-element.97, bf16[4096,2048]{1,0:T(8,128)(2,1)} %all-gather.11.cloned.1.call-done, s32[]{:T(128)S(6)} %select_n.200), kind=kOutput, calls=%fused_computation.19 | convolution fusion | flops 11542724608 | bytes 25296900 | tf_op jit(solution)/shard_map/dot_general | solution.py:28
  1284.7 7.8 reshape.193
  1292.4 7.8 reshape.196
  1300.2 25.8 %constant_dynamic-slice_fusion = (f32[1,256,1376]{1,0,2:T(1,128)S(1)}, f32[1,256,1376]{1,0,2:T(1,128)S(1)}, f32[1,256,1376]{1,0,2:T(1,128)S(1)}, f32[1,256,1376]...) fusion(f32[4,256,1376]{1,0,2:T(4,128)} %reshape.196, ...), kind=kLoop, calls=%fused_computation.151 | loop fusion | bytes 22544400 | tf_op jit(solution)/shard_map/jit(dynamic_index_in_dim)/dynamic_slice | solution.py:176
  1336.2 13.6 fusion.54
  1349.8 14.5 convolution_add_fusion.1
  1364.3 7.7 dynamic-slice_bitcast_fusion
  1372.0 18.8 %fusion.17 = f32[688,2048]{1,0:T(8,128)} fusion(bf16[4096,2048]{1,0:T(8,128)(2,1)} %all-gather.13.cloned.1.call-done, bf16[4096,1376]{0,1:T(8,128)(2,1)} %get-tuple-element.96, s32[]{:T(128)S(6)} %select_n.201), kind=kOutput, calls=%fused_computation.40 | convolution fusion | flops 11542724608 | bytes 28049412 | tf_op jit(solution)/shard_map/dot_general | solution.py:28
  1413.0 6.7 fusion.81
  1422.3 11.7 bitcast_add_fusion
  1440.7 9.7 fusion.82
  1450.5 37.0 %all-to-all-done.2 = f32[8,256,256]{2,1,0:T(8,128)S(1)} async-done(((f32[8,256,256]{2,1,0:T(8,128)}), f32[8,256,256]{2,1,0:T(8,128)S(1)}, u32[]{:S(2)}, u32[]{:S(2)}) %all-to-all-start.2) | async-done | bytes 2097184 | tf_op jit(solution)/shard_map/all_to_all | solution.py:327
  1505.0 9.6 fusion.83
  1514.7 84.9 %all-to-all-done.3 = f32[8,256,256]{2,1,0:T(8,128)} async-done(((f32[8,256,256]{2,1,0:T(8,128)}), f32[8,256,256]{2,1,0:T(8,128)}, u32[]{:S(2)}, u32[]{:S(2)}) %all-to-all-start.3) | async-done | bytes 2097184 | tf_op jit(solution)/shard_map/all_to_all | solution.py:327
  1617.3 9.6 fusion.84
  (350 shorter events, 345.2 us)
Async XLA Ops:
  7.2 227.0 %all-gather.7.cloned.1.call-start = ((), (), s32[]{:S(2)}) async-start(), calls=%async_computation.5 | async-start | bytes 18874368 | tf_op jit(solution)/shard_map/all_gather | solution.py:170
  29.3 322.9 %all-gather.9.cloned.1.call-start = ((), (), s32[]{:S(2)}) async-start(), calls=%async_computation.6 | async-start | bytes 9437184 | tf_op jit(solution)/shard_map/all_gather | solution.py:170
  30.1 642.3 %all-gather.13.cloned.1.call-start = ((), (), s32[]{:S(2)}) async-start(), calls=%async_computation.8 | async-start | bytes 18874368 | tf_op jit(solution)/shard_map/all_gather | solution.py:170
  38.8 9.0 collective-permute-start
  41.1 36.9 %collective-permute-start.1 = (bf16[256,1536]{1,0:T(8,128)(2,1)}, bf16[256,1536]{1,0:T(8,128)(2,1)}, u32[]{:S(2)}, u32[]{:S(2)}) collective-permute-start(bf16[256,1536]{1,0:T(8,128)(2,1)} %bitcast.7), channel_id=1, source_target_pairs={{0,2},{1,3},{2,0},{3,1},{4,6},{5,7},{6,4},{7,5}} | collective-permute-start | bytes 2359304 | tf_op jit(solution)/shard_map/ppermute | solution.py:173
  43.9 61.1 %collective-permute-start.2 = (bf16[256,1536]{1,0:T(8,128)(2,1)}, bf16[256,1536]{1,0:T(8,128)(2,1)}, u32[]{:S(2)}, u32[]{:S(2)}) collective-permute-start(bf16[256,1536]{1,0:T(8,128)(2,1)} %bitcast.9), channel_id=1, source_target_pairs={{0,3},{1,2},{2,1},{3,0},{4,7},{5,6},{6,5},{7,4}} | collective-permute-start | bytes 2359304 | tf_op jit(solution)/shard_map/ppermute | solution.py:173
  107.6 56.8 %collective-permute-start.18 = (bf16[1024,768]{1,0:T(8,128)(2,1)}, bf16[1024,768]{1,0:T(8,128)(2,1)}, u32[]{:S(2)}, u32[]{:S(2)}) collective-permute-start(bf16[1024,768]{1,0:T(8,128)(2,1)} %constant_dynamic-slice_fusion.12), channel_id=1, source_target_pairs={{0,4},{1,5},{2,6},{3,7},{4,0},{5,1},{6,2},{7,3}} | collective-permute-start | bytes 4718600 | tf_op jit(solution)/shard_map/ppermute | solution.py:173
  166.6 63.5 %collective-permute-start.3 = (bf16[1024,768]{1,0:T(8,128)(2,1)}, bf16[1024,768]{1,0:T(8,128)(2,1)}, u32[]{:S(2)}, u32[]{:S(2)}) collective-permute-start(bf16[1024,768]{1,0:T(8,128)(2,1)} %get-tuple-element.93), channel_id=1, source_target_pairs={{0,4},{1,5},{2,6},{3,7},{4,0},{5,1},{6,2},{7,3}} | collective-permute-start | bytes 4718600 | tf_op jit(solution)/shard_map/ppermute | solution.py:173
  168.5 120.1 %copy-start.16 = (s32[16]{0:T(128)}, s32[16]{0:T(128)S(1)}, u32[]{:S(2)}) copy-start(s32[16]{0:T(128)S(1)} %and_select_fusion.lo_ref) | copy-start | bytes 196
  168.6 120.1 %copy-start.14 = (s32[16,1,256]{2,1,0:T(1,128)}, s32[16,1,256]{2,1,0:T(1,128)S(1)}, u32[]{:S(2)}) copy-start(s32[16,1,256]{2,1,0:T(1,128)S(1)} %add_subtract_fusion.start_ref) | copy-start | bytes 49156
  172.3 100.1 %copy-start.24 = (f32[4096,64]{0,1:T(8,128)}, f32[4096,64]{0,1:T(8,128)S(1)}, u32[]{:S(2)}) copy-start(f32[4096,64]{0,1:T(8,128)S(1)} %get-tuple-element.148) | copy-start | bytes 3145732
  172.3 100.0 %copy-start.26 = (f32[4096,64]{0,1:T(8,128)}, f32[4096,64]{0,1:T(8,128)S(1)}, u32[]{:S(2)}) copy-start(f32[4096,64]{0,1:T(8,128)S(1)} %get-tuple-element.149) | copy-start | bytes 3145732
  348.9 29.6 %all-to-all-start = ((bf16[8,512,256]{1,2,0:T(8,128)(2,1)}), bf16[8,512,256]{1,2,0:T(8,128)(2,1)}, u32[]{:S(2)}, u32[]{:S(2)}) async-start(bf16[8,512,256]{1,2,0:T(8,128)(2,1)} %copy.243), calls=%async_computation | async-start | bytes 4194304 | tf_op jit(solution)/shard_map/all_to_all | solution.py:251
  352.0 350.7 %all-gather.11.cloned.1.call-start = ((), (), s32[]{:S(2)}) async-start(), calls=%async_computation.7 | async-start | bytes 18874368 | tf_op jit(solution)/shard_map/all_gather | solution.py:170
  391.3 746.8 %all-gather.15.cloned.1.call-start = ((), (), s32[]{:S(2)}) async-start(), calls=%async_computation.9 | async-start | bytes 18874368 | tf_op jit(solution)/shard_map/all_gather | solution.py:170
  396.8 11.2 collective-permute-start.4
  396.8 33.8 %collective-permute-start.5 = (bf16[256,1376]{0,1:T(8,128)(2,1)}, bf16[256,1376]{0,1:T(8,128)(2,1)}, u32[]{:S(2)}, u32[]{:S(2)}) collective-permute-start(bf16[256,1376]{0,1:T(8,128)(2,1)} %get-tuple-element.131), channel_id=1, source_target_pairs={{0,2},{1,3},{2,0},{3,1},{4,6},{5,7},{6,4},{7,5}} | collective-permute-start | bytes 2113544 | tf_op jit(solution)/shard_map/ppermute | solution.py:173
  396.9 57.4 %collective-permute-start.6 = (bf16[256,1376]{0,1:T(8,128)(2,1)}, bf16[256,1376]{0,1:T(8,128)(2,1)}, u32[]{:S(2)}, u32[]{:S(2)}) collective-permute-start(bf16[256,1376]{0,1:T(8,128)(2,1)} %get-tuple-element.130), channel_id=1, source_target_pairs={{0,3},{1,2},{2,1},{3,0},{4,7},{5,6},{6,5},{7,4}} | collective-permute-start | bytes 2113544 | tf_op jit(solution)/shard_map/ppermute | solution.py:173
  404.2 62.9 %collective-permute-start.8 = (bf16[256,1376]{0,1:T(8,128)(2,1)}, bf16[256,1376]{0,1:T(8,128)(2,1)}, u32[]{:S(2)}, u32[]{:S(2)}) collective-permute-start(bf16[256,1376]{0,1:T(8,128)(2,1)} %get-tuple-element.136), channel_id=1, source_target_pairs={{0,1},{1,0},{2,3},{3,2},{4,5},{5,4},{6,7},{7,6}} | collective-permute-start | bytes 2113544 | tf_op jit(solution)/shard_map/ppermute | solution.py:173
  404.5 80.8 %collective-permute-start.9 = (bf16[256,1376]{0,1:T(8,128)(2,1)}, bf16[256,1376]{0,1:T(8,128)(2,1)}, u32[]{:S(2)}, u32[]{:S(2)}) collective-permute-start(bf16[256,1376]{0,1:T(8,128)(2,1)} %get-tuple-element.135), channel_id=1, source_target_pairs={{0,2},{1,3},{2,0},{3,1},{4,6},{5,7},{6,4},{7,5}} | collective-permute-start | bytes 2113544 | tf_op jit(solution)/shard_map/ppermute | solution.py:173
  408.0 106.8 %collective-permute-start.10 = (bf16[256,1376]{0,1:T(8,128)(2,1)}, bf16[256,1376]{0,1:T(8,128)(2,1)}, u32[]{:S(2)}, u32[]{:S(2)}) collective-permute-start(bf16[256,1376]{0,1:T(8,128)(2,1)} %get-tuple-element.134), channel_id=1, source_target_pairs={{0,3},{1,2},{2,1},{3,0},{4,7},{5,6},{6,5},{7,4}} | collective-permute-start | bytes 2113544 | tf_op jit(solution)/shard_map/ppermute | solution.py:173
  430.6 108.7 %collective-permute-start.12 = (bf16[688,2048]{1,0:T(8,128)(2,1)}, bf16[688,2048]{1,0:T(8,128)(2,1)}, u32[]{:S(2)}, u32[]{:S(2)}) collective-permute-start(bf16[688,2048]{1,0:T(8,128)(2,1)} %param.24), channel_id=1, source_target_pairs={{0,4},{1,5},{2,6},{3,7},{4,0},{5,1},{6,2},{7,3}} | collective-permute-start | bytes 8454152 | tf_op jit(solution)/shard_map/ppermute | solution.py:173
  467.1 132.7 %collective-permute-start.7 = (bf16[1024,1376]{0,1:T(8,128)(2,1)}, bf16[1024,1376]{0,1:T(8,128)(2,1)}, u32[]{:S(2)}, u32[]{:S(2)}) collective-permute-start(bf16[1024,1376]{0,1:T(8,128)(2,1)} %copy.250), channel_id=1, source_target_pairs={{0,4},{1,5},{2,6},{3,7},{4,0},{5,1},{6,2},{7,3}} | collective-permute-start | bytes 8454152 | tf_op jit(solution)/shard_map/ppermute | solution.py:173
  523.3 135.4 %collective-permute-start.11 = (bf16[1024,1376]{0,1:T(8,128)(2,1)}, bf16[1024,1376]{0,1:T(8,128)(2,1)}, u32[]{:S(2)}, u32[]{:S(2)}) collective-permute-start(bf16[1024,1376]{0,1:T(8,128)(2,1)} %copy.259), channel_id=1, source_target_pairs={{0,4},{1,5},{2,6},{3,7},{4,0},{5,1},{6,2},{7,3}} | collective-permute-start | bytes 8454152 | tf_op jit(solution)/shard_map/ppermute | solution.py:173
  824.4 26.4 %collective-permute-start.15 = (f32[2,512,2048]{2,1,0:T(8,128)}, f32[2,512,2048]{2,1,0:T(8,128)}, u32[]{:S(2)}, u32[]{:S(2)}) collective-permute-start(f32[2,512,2048]{2,1,0:T(8,128)} %dynamic-slice_bitcast_fusion.1), channel_id=1, source_target_pairs={{0,1},{1,0},{2,3},{3,2},{4,5},{5,4},{6,7},{7,6}} | collective-permute-start | bytes 25165832 | tf_op jit(solution)/shard_map/ppermute | solution.py:173
  850.2 17.3 %collective-permute-start.13 = (f32[2,512,2048]{2,1,0:T(8,128)}, f32[2,512,2048]{2,1,0:T(8,128)}, u32[]{:S(2)}, u32[]{:S(2)}) collective-permute-start(f32[2,512,2048]{2,1,0:T(8,128)} %dynamic-slice_bitcast_fusion.2), channel_id=1, source_target_pairs={{0,1},{1,0},{2,3},{3,2},{4,5},{5,4},{6,7},{7,6}} | collective-permute-start | bytes 25165832 | tf_op jit(solution)/shard_map/ppermute | solution.py:173
  867.1 93.4 %collective-permute-start.16 = (f32[512,2048]{1,0:T(8,128)}, f32[512,2048]{1,0:T(8,128)}, u32[]{:S(2)}, u32[]{:S(2)}) collective-permute-start(f32[512,2048]{1,0:T(8,128)} %dynamic-slice_bitcast_fusion.4), channel_id=1, source_target_pairs={{0,2},{1,3},{2,0},{3,1},{4,6},{5,7},{6,4},{7,5}} | collective-permute-start | bytes 12582920 | tf_op jit(solution)/shard_map/ppermute | solution.py:173
  879.2 81.3 %copy-start.31 = (bf16[512,2048]{1,0:T(8,128)(2,1)S(1)}, bf16[512,2048]{1,0:T(8,128)(2,1)}, u32[]{:S(2)}) copy-start(bf16[512,2048]{1,0:T(8,128)(2,1)} %copy-done.30) | copy-start | bytes 6291460
  879.2 81.3 %copy-start.65 = (f32[1,2,8,128]{3,1,2,0:T(2,128)S(1)}, f32[1,2,8,128]{3,1,2,0:T(2,128)}, u32[]{:S(2)}) copy-start(f32[1,2,8,128]{3,1,2,0:T(2,128)} %copy-done.64) | copy-start | bytes 24580
  879.2 81.3 %copy-start.69 = (f32[512]{0:T(512)S(1)}, f32[512]{0:T(512)}, u32[]{:S(2)}) copy-start(f32[512]{0:T(512)} %copy-done.68) | copy-start | bytes 6148
  884.1 165.4 %collective-permute-start.14 = (f32[512,2048]{1,0:T(8,128)}, f32[512,2048]{1,0:T(8,128)}, u32[]{:S(2)}, u32[]{:S(2)}) collective-permute-start(f32[512,2048]{1,0:T(8,128)} %dynamic-slice_bitcast_fusion.5), channel_id=1, source_target_pairs={{0,2},{1,3},{2,0},{3,1},{4,6},{5,7},{6,4},{7,5}} | collective-permute-start | bytes 12582920 | tf_op jit(solution)/shard_map/ppermute | solution.py:173
  885.7 163.8 %copy-start.22 = (f32[2,512,2048]{2,1,0:T(8,128)S(1)}, f32[2,512,2048]{2,1,0:T(8,128)}, u32[]{:S(2)}) copy-start(f32[2,512,2048]{2,1,0:T(8,128)} %bitcast_add_fusion.2) | copy-start | bytes 25165828
  885.7 163.8 %copy-start.42 = (bf16[512,2048]{1,0:T(8,128)(2,1)S(1)}, bf16[512,2048]{1,0:T(8,128)(2,1)}, u32[]{:S(2)}) copy-start(bf16[512,2048]{1,0:T(8,128)(2,1)} %param.15) | copy-start | bytes 6291460
  1057.7 80.4 %copy-start.1 = (bf16[4096,256]{1,0:T(8,128)(2,1)S(1)}, bf16[4096,256]{1,0:T(8,128)(2,1)}, u32[]{:S(2)}) copy-start(bf16[4096,256]{1,0:T(8,128)(2,1)} %copy-done) | copy-start | bytes 6291460
  1057.7 80.4 %copy-start.61 = (bf16[2,128,2048]{2,1,0:T(8,128)(2,1)S(1)}, bf16[2,128,2048]{2,1,0:T(8,128)(2,1)}, u32[]{:S(2)}) copy-start(bf16[2,128,2048]{2,1,0:T(8,128)(2,1)} %param.20) | copy-start | bytes 3145732
  1265.9 70.3 %collective-permute-start.17 = (bf16[2048,768]{0,1:T(8,128)(2,1)}, bf16[2048,768]{0,1:T(8,128)(2,1)}, u32[]{:S(2)}, u32[]{:S(2)}) collective-permute-start(bf16[2048,768]{0,1:T(8,128)(2,1)} %constant_dynamic-slice_fusion.8), channel_id=1, source_target_pairs={{0,4},{1,5},{2,6},{3,7},{4,0},{5,1},{6,2},{7,3}} | collective-permute-start | bytes 9437192 | tf_op jit(solution)/shard_map/ppermute | solution.py:173
  1327.2 73.6 %collective-permute-start.24 = (f32[256,1376]{0,1:T(8,128)}, f32[256,1376]{0,1:T(8,128)}, u32[]{:S(2)}, u32[]{:S(2)}) collective-permute-start(f32[256,1376]{0,1:T(8,128)} %bitcast.184), channel_id=1, source_target_pairs={{0,1},{1,0},{2,3},{3,2},{4,5},{5,4},{6,7},{7,6}} | collective-permute-start | bytes 4227080 | tf_op jit(solution)/shard_map/ppermute | solution.py:173
  1328.4 76.4 %collective-permute-start.25 = (f32[256,1376]{0,1:T(8,128)}, f32[256,1376]{0,1:T(8,128)}, u32[]{:S(2)}, u32[]{:S(2)}) collective-permute-start(f32[256,1376]{0,1:T(8,128)} %bitcast.183), channel_id=1, source_target_pairs={{0,2},{1,3},{2,0},{3,1},{4,6},{5,7},{6,4},{7,5}} | collective-permute-start | bytes 4227080 | tf_op jit(solution)/shard_map/ppermute | solution.py:173
  1330.9 77.0 %collective-permute-start.26 = (f32[256,1376]{0,1:T(8,128)}, f32[256,1376]{0,1:T(8,128)}, u32[]{:S(2)}, u32[]{:S(2)}) collective-permute-start(f32[256,1376]{0,1:T(8,128)} %bitcast.182), channel_id=1, source_target_pairs={{0,3},{1,2},{2,1},{3,0},{4,7},{5,6},{6,5},{7,4}} | collective-permute-start | bytes 4227080 | tf_op jit(solution)/shard_map/ppermute | solution.py:173
  1332.7 77.8 %collective-permute-start.21 = (f32[256,1376]{0,1:T(8,128)}, f32[256,1376]{0,1:T(8,128)}, u32[]{:S(2)}, u32[]{:S(2)}) collective-permute-start(f32[256,1376]{0,1:T(8,128)} %bitcast.187), channel_id=1, source_target_pairs={{0,1},{1,0},{2,3},{3,2},{4,5},{5,4},{6,7},{7,6}} | collective-permute-start | bytes 4227080 | tf_op jit(solution)/shard_map/ppermute | solution.py:173
  1372.0 50.3 %collective-permute-start.19 = (f32[2,512,2048]{2,1,0:T(8,128)}, f32[2,512,2048]{2,1,0:T(8,128)}, u32[]{:S(2)}, u32[]{:S(2)}) collective-permute-start(f32[2,512,2048]{2,1,0:T(8,128)} %dynamic-slice_bitcast_fusion), channel_id=1, source_target_pairs={{0,1},{1,0},{2,3},{3,2},{4,5},{5,4},{6,7},{7,6}} | collective-permute-start | bytes 25165832 | tf_op jit(solution)/shard_map/ppermute | solution.py:173
  1400.9 89.8 %collective-permute-start.22 = (f32[256,1376]{0,1:T(8,128)}, f32[256,1376]{0,1:T(8,128)}, u32[]{:S(2)}, u32[]{:S(2)}) collective-permute-start(f32[256,1376]{0,1:T(8,128)} %bitcast.186), channel_id=1, source_target_pairs={{0,2},{1,3},{2,0},{3,1},{4,6},{5,7},{6,4},{7,5}} | collective-permute-start | bytes 4227080 | tf_op jit(solution)/shard_map/ppermute | solution.py:173
  1404.9 198.0 %collective-permute-start.23 = (f32[256,1376]{0,1:T(8,128)S(1)}, f32[256,1376]{0,1:T(8,128)}, u32[]{:S(2)}, u32[]{:S(2)}) collective-permute-start(f32[256,1376]{0,1:T(8,128)S(1)} %bitcast.220), channel_id=1, source_target_pairs={{0,3},{1,2},{2,1},{3,0},{4,7},{5,6},{6,5},{7,4}} | collective-permute-start | bytes 4227080 | tf_op jit(solution)/shard_map/ppermute | solution.py:173
  1419.7 67.8 %all-to-all-start.2 = ((f32[8,256,256]{2,1,0:T(8,128)}), f32[8,256,256]{2,1,0:T(8,128)S(1)}, u32[]{:S(2)}, u32[]{:S(2)}) async-start(f32[8,256,256]{2,1,0:T(8,128)} %bitcast.219), calls=%async_computation.2 | async-start | bytes 4194304 | tf_op jit(solution)/shard_map/all_to_all | solution.py:327
  1438.8 201.8 %collective-permute-start.20 = (f32[512,2048]{1,0:T(8,128)}, f32[512,2048]{1,0:T(8,128)}, u32[]{:S(2)}, u32[]{:S(2)}) collective-permute-start(f32[512,2048]{1,0:T(8,128)} %dynamic-slice_bitcast_fusion.3), channel_id=1, source_target_pairs={{0,2},{1,3},{2,0},{3,1},{4,6},{5,7},{6,4},{7,5}} | collective-permute-start | bytes 12582920 | tf_op jit(solution)/shard_map/ppermute | solution.py:173
  1487.5 112.1 %all-to-all-start.3 = ((f32[8,256,256]{2,1,0:T(8,128)}), f32[8,256,256]{2,1,0:T(8,128)}, u32[]{:S(2)}, u32[]{:S(2)}) async-start(f32[8,256,256]{2,1,0:T(8,128)} %bitcast.218), calls=%async_computation.3 | async-start | bytes 4194304 | tf_op jit(solution)/shard_map/all_to_all | solution.py:327
  1599.6 34.2 %all-to-all-start.4 = ((f32[8,256,256]{2,1,0:T(8,128)}), f32[8,256,256]{2,1,0:T(8,128)}, u32[]{:S(2)}, u32[]{:S(2)}) async-start(f32[8,256,256]{2,1,0:T(8,128)} %bitcast.217), calls=%async_computation.4 | async-start | bytes 4194304 | tf_op jit(solution)/shard_map/all_to_all | solution.py:327
  1647.3 7.9 all-to-all-start.1
  (66 other events, 624.5 us)
Sparse Core Ops, SparseCore 0:
  29.5 120.3 all-gather.6
  151.7 78.5 all-gather.8
  232.1 84.0 all-gather.12
  391.4 150.8 all-gather.10
  1055.0 83.0 all-gather.14

commit v2 on v1

v2 whole, which is shorter than its diff:
```python
import functools

import jax
import jax.numpy as jnp
from jax import lax
from jax.experimental import pallas as pl
from jax.experimental.pallas import tpu as pltpu
from jax.sharding import PartitionSpec as P

NORM_EPS = 1e-5
ROPE_BASE = 10000.0
BF = jnp.bfloat16
F32 = jnp.float32
HD = 128
BT = 256
BQ = 256
BK = 512
NEG = -1e30
SIB, XN, YN = 1, 2, 4


def dot(a, b):
    return lax.dot_general(a, b, (((1,), (0,)), ((), ())), preferred_element_type=F32)


def dot_nt(a, b):
    return lax.dot_general(a, b, (((1,), (1,)), ((), ())), preferred_element_type=F32)


def dot_tn(a, b):
    return lax.dot_general(a, b, (((0,), (0,)), ((), ())), preferred_element_type=F32)


def head_cols(h):
    return slice(h * HD, (h + 1) * HD)


def qkv_kernel(x_ref, gain_ref, w_ref, cos_ref, sin_ref, u_ref, q_ref, k_ref, v_ref, kt_ref, vt_ref):
    xw = x_ref[...].astype(F32)
    inv = lax.rsqrt(jnp.mean(xw * xw, axis=-1, keepdims=True) + NORM_EPS)
    u = (xw * inv * gain_ref[...]).astype(BF)
    u_ref[...] = u
    cos, sin = cos_ref[...], sin_ref[...]
    width = q_ref.shape[1]
    for part, ref in ((0, q_ref), (1, k_ref), (2, v_ref)):
        t = dot(u, w_ref[:, part * width:(part + 1) * width])
        for h in range(width // HD):
            th = t[:, head_cols(h)]
            if part < 2:
                th = th * cos + pltpu.roll(th, HD // 2, 1) * sin
            tb = th.astype(BF)
            ref[:, head_cols(h)] = tb
            if part == 1:
                kt_ref[head_cols(h), :] = tb.astype(F32).T.astype(BF)
            if part == 2:
                vt_ref[head_cols(h), :] = tb.astype(F32).T.astype(BF)


def qkv_project(x_all, gain, w, cos, sin):
    tokens, d = x_all.shape
    width = w.shape[1] // 3
    row = lambda k: pl.BlockSpec((BT, k), lambda i: (i, 0))
    full = lambda a: pl.BlockSpec(a.shape, lambda i: (0, 0))
    col = pl.BlockSpec((width, BT), lambda i: (0, i))
    tok = jax.ShapeDtypeStruct((tokens, width), BF)
    tra = jax.ShapeDtypeStruct((width, tokens), BF)
    return pl.pallas_call(
        qkv_kernel, grid=(tokens // BT,),
        in_specs=[row(d), full(gain), full(w), row(HD), row(HD)],
        out_specs=[row(d), row(width), row(width), row(width), col, col],
        out_shape=[jax.ShapeDtypeStruct((tokens, d), BF), tok, tok, tok, tra, tra],
        compiler_params=pltpu.CompilerParams(dimension_semantics=("arbitrary",), vmem_limit_bytes=40 * 1024 * 1024),
        cost_estimate=pl.CostEstimate(flops=2 * tokens * d * 3 * width, bytes_accessed=50_000_000, transcendentals=0),
        name="qkv_proj",
    )(x_all, gain, w, cos, sin)


def fold(t, op):
    return op(t.reshape(t.shape[0] // 8, 8, t.shape[1]), axis=0)


def block_allowed(i, j, start_row):
    kv = lax.broadcasted_iota(jnp.int32, (BK, BQ), 0)
    top = i * BQ - j * BK + lax.broadcasted_iota(jnp.int32, (1, BQ), 1)
    return (kv <= top) & (kv >= start_row - j * BK)


def attn_fwd_kernel(scale, heads, lo_ref, q_ref, k_ref, vt_ref, start_ref, o_ref, lse_ref, s_scr):
    i = pl.program_id(0)
    lo = lo_ref[i]
    hi = (i * BQ + BQ - 1) // BK + 1
    start_row = start_ref[0]
    zero = tuple(jnp.zeros((8, BQ), F32) for _ in range(heads))

    def logits(j, ms):
        rows = pl.ds(pl.multiple_of(j * BK, BK), BK)
        ok = block_allowed(i, j, start_row)
        out = []
        for h in range(heads):
            s = dot_nt(k_ref[rows, head_cols(h)], q_ref[:, head_cols(h)]) * scale
            s = jnp.where(ok, s, NEG)
            s_scr[h, j] = s
            out.append(jnp.maximum(ms[h], fold(s, jnp.max)))
        return tuple(out)

    ms = lax.fori_loop(lo, hi, logits, tuple(z + NEG for z in zero))
    ms = [jnp.max(m, axis=0, keepdims=True) for m in ms]

    def exps(j, ls):
        out = []
        for h in range(heads):
            e = jnp.exp(s_scr[h, j] - ms[h])
            s_scr[h, j] = e
            out.append(ls[h] + fold(e, jnp.sum))
        return tuple(out)

    ls = lax.fori_loop(lo, hi, exps, zero)
    ls = [jnp.sum(l, axis=0, keepdims=True) for l in ls]
    inv = [1.0 / l for l in ls]
    for h in range(heads):
        lse_ref[0, h:h + 1, :] = ms[h] + jnp.log(ls[h])

    def values(j, accs):
        rows = pl.ds(pl.multiple_of(j * BK, BK), BK)
        return tuple(accs[h] + dot(vt_ref[head_cols(h), rows], (s_scr[h, j] * inv[h]).astype(BF))
                     for h in range(heads))

    accs = lax.fori_loop(lo, hi, values, tuple(jnp.zeros((HD, BQ), F32) for _ in range(heads)))
    for h in range(heads):
        o_ref[:, head_cols(h)] = accs[h].T.astype(BF)


def attn_forward(q, k, vt, starts):
    tokens, width = q.shape
    heads = width // HD
    nq = tokens // BQ
    grid_spec = pltpu.PrefetchScalarGridSpec(
        num_scalar_prefetch=1, grid=(nq,),
        in_specs=[pl.BlockSpec((BQ, width), lambda i, *_: (i, 0)),
                  pl.BlockSpec((tokens, width), lambda i, *_: (0, 0)),
                  pl.BlockSpec((width, tokens), lambda i, *_: (0, 0)),
                  pl.BlockSpec((1, 1, BQ), lambda i, *_: (i, 0, 0))],
        out_specs=[pl.BlockSpec((BQ, width), lambda i, *_: (i, 0)),
                   pl.BlockSpec((1, heads, BQ), lambda i, *_: (i, 0, 0))],
        scratch_shapes=[pltpu.VMEM((heads, tokens // BK, BK, BQ), F32)])
    return pl.pallas_call(
        functools.partial(attn_fwd_kernel, HD ** -0.5, heads),
        grid_spec=grid_spec,
        out_shape=[jax.ShapeDtypeStruct((tokens, width), BF),
                   jax.ShapeDtypeStruct((nq, heads, BQ), F32)],
        compiler_params=pltpu.CompilerParams(dimension_semantics=("arbitrary",), vmem_limit_bytes=40 * 1024 * 1024),
        cost_estimate=pl.CostEstimate(flops=40_000_000_000, bytes_accessed=10_000_000, transcendentals=10_000_000),
        name="attn_fwd",
    )(starts[::BQ] // BK, q, k, vt, starts.reshape(nq, 1, BQ))


def attn_bwd_kernel(scale, heads, lo_ref, q_ref, do_ref, o_ref, k_ref, v_ref, kt_ref, lse_ref, start_ref,
                    cosq_ref, sinq_ref, cos_ref, sin_ref, dq_ref, dk_ref, dv_ref, dk_acc, dv_acc):
    i = pl.program_id(0)
    lo = lo_ref[i]
    hi = (i * BQ + BQ - 1) // BK + 1

    def rope_back(t, cos, sin):
        return (t * cos - pltpu.roll(t, HD // 2, 1) * sin).astype(BF)

    @pl.when(i == 0)
    def _():
        dk_acc[...] = jnp.zeros_like(dk_acc)
        dv_acc[...] = jnp.zeros_like(dv_acc)

    start_row = start_ref[0]
    delta = []
    for h in range(heads):
        prod = do_ref[:, head_cols(h)].astype(F32) * o_ref[:, head_cols(h)].astype(F32)
        delta.append(jnp.sum(prod.T, axis=0, keepdims=True))

    def body(j, dqts):
        rows = pl.ds(pl.multiple_of(j * BK, BK), BK)
        ok = block_allowed(i, j, start_row)
        out = []
        for h in range(heads):
            c = head_cols(h)
            q = q_ref[:, c]
            do = do_ref[:, c]
            s = dot_nt(k_ref[rows, c], q) * scale
            p = jnp.where(ok, jnp.exp(s - lse_ref[0, h:h + 1, :]), 0.0)
            dv_acc[rows, c] += dot(p.astype(BF), do)
            dp = dot_nt(v_ref[rows, c], do).astype(BF).astype(F32)
            ds = (p * (dp - delta[h]) * scale).astype(BF)
            dk_acc[rows, c] += dot(ds, q)
            out.append(dqts[h] + dot(kt_ref[c, rows], ds))
        return tuple(out)

    dqts = lax.fori_loop(lo, hi, body, tuple(jnp.zeros((HD, BQ), F32) for _ in range(heads)))
    for h in range(heads):
        dq = dqts[h].T.astype(BF).astype(F32)
        dq_ref[:, head_cols(h)] = rope_back(dq, cosq_ref[...], sinq_ref[...])

    @pl.when(i == pl.num_programs(0) - 1)
    def _():
        def finish(b, carry):
            rows = pl.ds(pl.multiple_of(b * BK, BK), BK)
            for h in range(heads):
                c = head_cols(h)
                dk = dk_acc[rows, c].astype(BF).astype(F32)
                dk_ref[rows, c] = rope_back(dk, cos_ref[rows, :], sin_ref[rows, :])
                dv_ref[rows, c] = dv_acc[rows, c].astype(BF)
            return carry

        lax.fori_loop(0, dk_acc.shape[0] // BK, finish, 0)


def attn_backward(q, k, v, kt, grad_o, o, lse, starts, cos, sin):
    tokens, width = q.shape
    heads = width // HD
    nq = tokens // BQ
    row = lambda w: pl.BlockSpec((BQ, w), lambda i, *_: (i, 0))
    full = lambda a: pl.BlockSpec(a, lambda i, *_: (0, 0))
    stat = lambda r: pl.BlockSpec((1, r, BQ), lambda i, *_: (i, 0, 0))
    grid_spec = pltpu.PrefetchScalarGridSpec(
        num_scalar_prefetch=1, grid=(nq,),
        in_specs=[row(width), row(width), row(width), full((tokens, width)), full((tokens, width)),
                  full((width, tokens)), stat(heads), stat(1), row(HD), row(HD), full((tokens, HD)), full((tokens, HD))],
        out_specs=[row(width), full((tokens, width)), full((tokens, width))],
        scratch_shapes=[pltpu.VMEM((tokens, width), F32), pltpu.VMEM((tokens, width), F32)])
    out = jax.ShapeDtypeStruct((tokens, width), BF)
    return pl.pallas_call(
        functools.partial(attn_bwd_kernel, HD ** -0.5, heads),
        grid_spec=grid_spec,
        out_shape=[out, out, out],
        compiler_params=pltpu.CompilerParams(dimension_semantics=("arbitrary",), vmem_limit_bytes=48 * 1024 * 1024),
        cost_estimate=pl.CostEstimate(flops=60_000_000_000, bytes_accessed=20_000_000, transcendentals=10_000_000),
        name="attn_bwd",
    )(starts[::BQ] // BK, q, grad_o, o, k, v, kt, lse, starts.reshape(nq, 1, BQ), cos, sin, cos, sin)


def rms_back(grad_out, normed, inv_rms):
    mean_term = jnp.mean(grad_out * normed, axis=-1, keepdims=True)
    return inv_rms * (grad_out - normed * mean_term)


def solution(mesh):
    row_spec = P('sp', None)
    cube_spec = P('sp', None, None)
    vec_spec = P('sp')
    n = mesh.shape['sp']
    same_y = [list(range(n // 2)), list(range(n // 2, n))]

    def gather(t):
        return lax.all_gather(t, 'sp', axis=0, tiled=True)

    def swap(t, mask):
        return lax.ppermute(t, 'sp', [(d, d ^ mask) for d in range(n)])

    def local_layer(x, seg_ids, positions, grad_y, norm1_gain, w_q, w_k, w_v, w_o, norm2_gain, w_gate, w_up, w_down):
        tl, d = x.shape
        tokens = tl * n
        dr = w_gate.shape[0]
        ff = w_gate.shape[1]
        fr = w_down.shape[0]
        hw = d // n
        me = lax.axis_index('sp')
        yy = me // 4

        with jax.named_scope("gx"):
            x_all = gather(x)
        with jax.named_scope("gsmall"):
            small = gather(jnp.concatenate([norm1_gain.astype(F32), norm2_gain.astype(F32),
                                            positions.astype(F32)])[None])
        gain1 = small[:, :dr].reshape(1, -1)
        gain2 = small[:, dr:2 * dr].reshape(1, -1)
        pos_all = small[:, 2 * dr:].reshape(-1)
        starts = jnp.arange(tokens, dtype=jnp.int32) - pos_all.astype(jnp.int32)

        half = HD // 2
        inv_freq = ROPE_BASE ** (-jnp.arange(half, dtype=F32) * 2.0 / HD)
        angle = pos_all[:, None] * inv_freq[None, :]
        cos_t, sin_t = jnp.cos(angle), jnp.sin(angle)
        cos_full = jnp.concatenate([cos_t, cos_t], axis=-1)
        sin_full = jnp.concatenate([-sin_t, sin_t], axis=-1)

        with jax.named_scope("wqkv"):
            wqkv = jnp.stack([w.reshape(dr, n, hw) for w in (w_q, w_k, w_v)], axis=2).reshape(dr, -1)
            w_own = lax.all_to_all(wqkv, 'sp', 1, 0, tiled=True)

        def half_tokens(t, name):
            with jax.named_scope(name + "_x"):
                pair = jnp.concatenate([t, swap(t, XN)], axis=0)
            with jax.named_scope(name + "_s"):
                return pair, jnp.concatenate([pair, swap(pair, SIB)], axis=0)

        def other_half(pair, name):
            with jax.named_scope(name + "_y"):
                far = swap(pair, YN)
            with jax.named_scope(name + "_ys"):
                return jnp.concatenate([far, swap(far, SIB)], axis=0)

        gy_pair, gy_half = half_tokens(grad_y, "gy")

        with jax.named_scope("wd"):
            far = swap(w_down, YN)
            wd_quarter = jnp.concatenate([jnp.where(yy == 0, w_down, far), jnp.where(yy == 0, far, w_down)], axis=0)

        def ff_quarter(w):
            w4 = w.reshape(dr, 2, 4, fr).transpose(0, 2, 1, 3).reshape(dr, 4 * 2 * fr)
            return lax.all_to_all(jnp.concatenate([w4, w4], axis=1), 'sp', 1, 0, tiled=True)

        with jax.named_scope("wg"):
            wg_quarter = ff_quarter(w_gate)
        with jax.named_scope("wu"):
            wu_quarter = ff_quarter(w_up)

        with jax.named_scope("qkv"):
            u_all, q, k, v, kt, vt = qkv_project(x_all, gain1, w_own, cos_full, sin_full)
        with jax.named_scope("attnf"):
            o, lse = attn_forward(q, k, vt, starts)

        with jax.named_scope("oloc"):
            o_loc = lax.all_to_all(o, 'sp', 0, 1, tiled=True)
        wo_own = w_o.reshape(hw, d)
        with jax.named_scope("gwo"):
            wo_full = gather(wo_own)
        x_wide = x.astype(F32)
        with jax.named_scope("oproj"):
            h_res = (x_wide + dot(o_loc, wo_full)).astype(BF)
        h_wide = h_res.astype(F32)
        inv_rms2 = lax.rsqrt(jnp.mean(h_wide * h_wide, axis=-1, keepdims=True) + NORM_EPS)
        normed2 = h_wide * inv_rms2
        z_norm = (normed2 * gain2).astype(BF)
        z_pair, z_half = half_tokens(z_norm, "z")

        def mlp(z, gy):
            grad_act = dot_nt(gy, wd_quarter).astype(BF).astype(F32)
            gate_pre = dot(z, wg_quarter)
            up_pre = dot(z, wu_quarter)
            gate_sig = jax.nn.sigmoid(gate_pre)
            gate_act = gate_pre * gate_sig
            mlp_act = (gate_act * up_pre).astype(BF)
            grad_gate = (grad_act * up_pre * gate_sig * (1.0 + gate_pre * (1.0 - gate_sig))).astype(BF)
            grad_up = (grad_act * gate_act).astype(BF)
            return mlp_act, grad_gate, grad_up

        def quarter_sum(near, far, name):
            with jax.named_scope(name + "_s"):
                kept = near + swap(far, SIB)
            with jax.named_scope(name + "_x"):
                return kept[:tl] + swap(kept[tl:], XN)

        with jax.named_scope("mlp1"):
            m1, gg1, gu1 = mlp(z_half, gy_half)
        with jax.named_scope("gzdot"):
            gz_far = dot_nt(gg1[2 * tl:], wg_quarter) + dot_nt(gu1[2 * tl:], wu_quarter)
            gz_near = dot_nt(gg1[:2 * tl], wg_quarter) + dot_nt(gu1[:2 * tl], wu_quarter)
        gz = quarter_sum(gz_near, gz_far, "gz")
        gz = gz.astype(BF).astype(F32)
        grad_gain2 = jnp.sum(gz * normed2, axis=0)
        grad_h = (grad_y.astype(F32) + rms_back(gz * gain2, normed2, inv_rms2)).astype(BF)
        with jax.named_scope("ggh"):
            gh_all = gather(grad_h)

        with jax.named_scope("ydot"):
            y_far = dot(m1[2 * tl:], wd_quarter)
            y_near = dot(m1[:2 * tl], wd_quarter)
        y = (h_wide + quarter_sum(y_near, y_far, "y")).astype(BF)

        z_oth = other_half(z_pair, "zo")
        gy_oth = other_half(gy_pair, "gyo")
        with jax.named_scope("mlp2"):
            m2, gg2, gu2 = mlp(z_oth, gy_oth)

        def cols(t, width, start):
            return lax.dynamic_slice_in_dim(t, start, width, 1)

        zc1 = cols(z_half, 4 * dr, yy * 4 * dr)
        zc2 = cols(z_oth, 4 * dr, yy * 4 * dr)

        def spread_rows(g):
            out = lax.all_to_all(g, 'sp', 0, 1, axis_index_groups=same_y, tiled=True)
            return out.reshape(dr, 4, 2, fr).transpose(0, 2, 1, 3).reshape(dr, ff)

        with jax.named_scope("gwg"):
            grad_wgate = spread_rows(dot_tn(zc1, gg1) + dot_tn(zc2, gg2))
        with jax.named_scope("gwu"):
            grad_wup = spread_rows(dot_tn(zc1, gu1) + dot_tn(zc2, gu2))
        with jax.named_scope("gwd"):
            grad_wdown = dot_tn(cols(m1, fr, yy * fr), gy_half) + dot_tn(cols(m2, fr, yy * fr), gy_oth)

        with jax.named_scope("gradodot"):
            grad_o = dot_nt(gh_all, wo_own).astype(BF)
        with jax.named_scope("attnb"):
            dq, dk, dv = attn_backward(q, k, v, kt, grad_o, o, lse, starts, cos_full, sin_full)
        dqkv = jnp.concatenate([dq, dk, dv], axis=1)

        def token_blocks(masks):
            return jnp.concatenate([lax.dynamic_slice_in_dim(dqkv, (me ^ m) * tl, tl, 0) for m in masks], axis=0)

        with jax.named_scope("woth"):
            w_oth = swap(w_own, YN)
        with jax.named_scope("doth"):
            d_oth = swap(token_blocks((4, 6, 5, 7)), YN)
        d_own = token_blocks((0, 2, 1, 3))
        with jax.named_scope("gudot"):
            u_far = dot_nt(d_own[2 * tl:], w_own) + dot_nt(d_oth[2 * tl:], w_oth)
            u_near = dot_nt(d_own[:2 * tl], w_own) + dot_nt(d_oth[:2 * tl], w_oth)
        gu = quarter_sum(u_near, u_far, "gu")
        gu = gu.astype(BF).astype(F32)

        with jax.named_scope("gwo"):
            grad_wo = dot_tn(o, gh_all)

        def spread_heads(g):
            return lax.all_to_all(g, 'sp', 0, 1, tiled=True)

        with jax.named_scope("gwqkv"):
            grad_wq = spread_heads(dot_tn(u_all, dq))
            grad_wk = spread_heads(dot_tn(u_all, dk))
            grad_wv = spread_heads(dot_tn(u_all, dv))

        inv_rms1 = lax.rsqrt(jnp.mean(x_wide * x_wide, axis=-1, keepdims=True) + NORM_EPS)
        normed1 = x_wide * inv_rms1
        grad_gain1 = jnp.sum(gu * normed1, axis=0)
        grad_x = (grad_h.astype(F32) + rms_back(gu * gain1, normed1, inv_rms1)).astype(BF)
        with jax.named_scope("gains"):
            gains = jnp.stack([grad_gain1.reshape(n, dr), grad_gain2.reshape(n, dr)], axis=1)
            gains = jnp.sum(lax.all_to_all(gains, 'sp', 0, 0, tiled=True), axis=0)
        return (y, grad_x, gains[0], grad_wq.reshape(w_q.shape), grad_wk.reshape(w_k.shape),
                grad_wv.reshape(w_v.shape), grad_wo.reshape(w_o.shape), gains[1], grad_wgate, grad_wup, grad_wdown)

    return jax.shard_map(
        local_layer, mesh=mesh,
        in_specs=(row_spec, vec_spec, vec_spec, row_spec, vec_spec, cube_spec, cube_spec, cube_spec, cube_spec,
                  vec_spec, row_spec, row_spec, row_spec),
        out_specs=(row_spec, row_spec, vec_spec, cube_spec, cube_spec, cube_spec, cube_spec, vec_spec,
                   row_spec, row_spec, row_spec),
        check_vma=False)
```

time: 1680 us -> 1540 us (0.917)
  local copies, waits for them, and re-layouts: 281 us -> 139 us
  blocking collectives: 13.8 us -> 147 us
  waiting for transfers between devices: 750 us -> 648 us
  other arithmetic: 136 us -> 63.9 us
  matrix products: 325 us -> 342 us
    all_gather x1, blocking collectives: 13.8 us -> 147 us  [gather(): return lax.all_gather(t, 'sp', axis=0, tiled=True)]
    all_to_all x3, waiting for transfers between devices: 122 us -> 56.6 us  [spread_heads(): return lax.all_to_all(g, 'sp', 0, 1, tiled=True)]
    all_gather x5 -> x3, waiting for transfers between devices: 62.1 us -> 0.02 us  [gather(): return lax.all_gather(t, 'sp', axis=0, tiled=True)]
    all_to_all x0 -> x5, waiting for transfers between devices: none -> 52.7 us  [the longest x2 37 us: spread_rows(): out = lax.all_to_all(g, 'sp', 0, 1, axis_index_groups=same_y, tiled=True)]
    squeeze x8 -> x0, local copies, waits for them, and re-layouts: 40.4 us -> none  [pick(): return lax.dynamic_index_in_dim(t, index, axis, keepdims=False)]
    dynamic_slice x10 -> x1, local copies, waits for them, and re-layouts: 40.5 us -> 1.59 us  [token_blocks(): lax.dynamic_slice_in_dim(dqkv, (me ^ m) * tl, tl, 0)]
    dynamic_update_slice x20 -> x0, local copies, waits for them, and re-layouts: 32.3 us -> none  [the longest x8 17.7 us: spread_rows(): out = lax.dynamic_update_slice(out, blocks[m][None], (qq ^ m, 0, 0))]
    reshape x6 -> x0, local copies, waits for them, and re-layouts: 30.7 us -> none  [the longest x2 15.5 us: spread_rows(): g4 = g.reshape(4, dr, 2 * fr)]
  transfers between devices with their start and end apart: 37 -> 30, of which waited for: 18 -> 13; matrix products, arithmetic and copies ran while one was open for 31% -> 29% of each run, Pallas kernels for 3% -> 8%
where the time goes in v2:
time: 1540 us; the launch traced here: 1530 us
  waiting for transfers between devices  648 us (42%)
  matrix products  342 us (22%)
  blocking collectives  147 us (10%)
  local copies, waits for them, and re-layouts  139 us (9%)
  Pallas kernels  123 us (8%)
  other arithmetic  63.9 us (4%)
  starting transfers between devices  49.5 us (3%)
    ppermute x17, waiting for transfers between devices, swap(): return lax.ppermute(t, 'sp', [(d, d ^ mask) for d in range(n)])  530 us
    all_gather x1, blocking collectives, gather(): return lax.all_gather(t, 'sp', axis=0, tiled=True)  147 us
    dot_general x11, matrix products, dot_nt(): lax.dot_general(a, b, (((1,), (1,)), ((), ())), preferred_element_type=F32)  119 us
    dot_general x7, matrix products, dot(): lax.dot_general(a, b, (((1,), (0,)), ((), ())), preferred_element_type=F32)  115 us
    dot_general x10, matrix products, dot_tn(): lax.dot_general(a, b, (((0,), (0,)), ((), ())), preferred_element_type=F32)  108 us
    pallas_call x1, Pallas kernels, attn_backward(): pl.pallas_call(functools.partial(attn_bwd_kernel, HD ** (-0.5), heads), g...  60.6 us
    all_to_all x3, waiting for transfers between devices, spread_heads(): return lax.all_to_all(g, 'sp', 0, 1, tiled=True)  56.6 us
    unnamed x127, local copies, waits for them, and re-layouts  51.7 us
  transfers between devices with their start and end apart: 30, of which 13 were waited for; matrix products, arithmetic and copies ran while one was open for 29% of the time, Pallas kernels for 8%

profile of v2, /device:TPU:0, one launch (start us, length us, event | category | flops | bytes accessed | tf_op | source)
XLA Modules:
  0.0 1527.9 jit_solution(10663427644798573687)
XLA Ops:
  21.3 147.5 %all-gather = f32[8192]{0:T(1024)S(1)} all-gather(f32[1024]{0:T(1024)S(1)} %pad_maximum_fusion.10), channel_id=2, replica_groups=mesh['sp'=8] {'sp'}, dimensions={0}, use_global_device_ids=true | all-gather | bytes 36864 | tf_op jit(solution)/shard_map/gsmall/all_gather | solution.py:250
  176.7 7.5 fusion.76
  194.9 27.5 %qkv_proj.1 = (bf16[4096,2048]{1,0:T(8,128)(2,1)}, bf16[4096,256]{1,0:T(8,128)(2,1)S(1)}, bf16[4096,256]{1,0:T(8,128)(2,1)S(1)}, bf16[4096,256]{1,0:T(8,128)(2,1...) custom-call(bf16[4096,2048]{1,0:T(8,128)(2,1)} %all-gather.5.cloned.1.call-done.x_ref, ...), custom_call_target="tpu_custom_call" | custom-call | flops 12884901888 | bytes 50000000 | tf_op jit(solution)/shard_map/qkv/qkv_proj/pallas_call | solution.py:67
  223.7 35.0 %attn_fwd.1 = (bf16[4096,256]{1,0:T(8,128)(2,1)S(1)}, f32[16,2,256]{2,1,0:T(2,128)S(1)}) custom-call(s32[16]{0:T(128)S(1)} %and_select_fusion.lo_ref, bf16[4096,256]{1,0:T(8,128)(2,1)S(1)} %get-tuple-element.22.q_ref, bf16[4096,256]{1,0:T(8,128)(2,1)S(1)} %get-tuple-element.23.k_ref, bf16[256,4096]{1,0:T(8,128)(2,1)S(1)} %get-tuple-element.24.vt_ref, ...), custom_call_target="tpu_custom_call" | custom-call | flops 40000000000 | bytes 10000000 | tf_op jit(solution)/shard_map/attnf/attn_fwd/pallas_call | solution.py:146
  261.4 15.7 %all-to-all-done.2 = bf16[256,8,1376]{0,2,1:T(8,128)(2,1)} async-done(((bf16[256,8,1376]{0,2,1:T(8,128)(2,1)}), bf16[256,8,1376]{0,2,1:T(8,128)(2,1)}, u32[]{:S(2)}, u32[]{:S(2)}) %all-to-all-start.2) | async-done | bytes 5636128 | tf_op jit(solution)/shard_map/wg/all_to_all | solution.py:306
  300.2 6.7 all-to-all-done.1
  310.5 9.1 fusion.43
  324.8 93.9 %collective-permute-done = bf16[512,2048]{1,0:T(8,128)(2,1)S(1)} collective-permute-done((bf16[512,2048]{1,0:T(8,128)(2,1)S(1)}, bf16[512,2048]{1,0:T(8,128)(2,1)S(1)}, u32[]{:S(2)}, u32[]{:S(2)}) %collective-permute-start) | collective-permute-done | bytes 2097184 | tf_op jit(solution)/shard_map/z_x/ppermute | solution.py:253
  422.5 11.5 collective-permute-done.2
  439.5 8.4 copy.112
  448.0 8.2 copy.115
  461.1 16.1 %convolution_convert_fusion.1 = bf16[2048,1376]{0,1:T(8,128)(2,1)} fusion(bf16[2048,2048]{1,0:T(8,128)(2,1)} %constant_dynamic-update-slice_fusion.2, bf16[688,2048]{1,0:T(8,128)(2,1)S(1)} %copy-done.22, bf16[688,2048]{1,0:T(8,128)(2,1)S(1)} %copy-done.19), kind=kOutput, calls=%fused_computation.21 | convolution fusion | flops 11556814848 | bytes 19660800 | tf_op jit(solution)/shard_map/mlp1/dot_general | solution.py:27
  477.2 19.2 %fusion.88 = f32[2048,1376]{0,1:T(8,128)} fusion(bf16[2048,1376]{1,0:T(8,128)(2,1)} %bitcast.110, bf16[1024,2048]{1,0:T(8,128)(2,1)} %collective-permute-done.1, bf16[512,2048]{1,0:T(8,128)(2,1)} %copy-done.16, bf16[512,2048]{1,0:T(8,128)(2,1)S(1)} %fusion.40), kind=kOutput, calls=%fused_computation.161 | convolution fusion | flops 11567890432 | bytes 25296896 | tf_op jit(solution)/shard_map/mlp1/dot_general | solution.py:23
  496.4 26.8 %fusion.2 = (bf16[2048,1376]{0,1:T(8,128)(2,1)}, bf16[2048,1376]{0,1:T(8,128)(2,1)}, bf16[2048,1376]{0,1:T(8,128)(2,1)}) fusion(bf16[2048,1376]{0,1:T(8,128)(2,1)} %convolution_convert_fusion.1, f32[2048,1376]{0,1:T(8,128)} %fusion.88, bf16[2048,1376]{1,0:T(8,128)(2,1)} %bitcast.116, bf16[1024,2048]{1,0:T(8,128)(2,1)} %collective-permute-done.1, ...), kind=kOutput, calls=%fused_computation.6 | convolution fusion | flops 11612979200 | bytes 47841280 | tf_op jit(solution)/shard_map/mlp1/dot_general | solution.py:23
  523.2 12.0 fusion.55
  535.2 13.2 convolution_add_fusion.1
  548.4 9.3 fusion.60
  558.2 9.1 fusion.58
  567.3 13.3 add_add_fusion.1
  584.1 11.3 convolution_add_fusion.2
  596.8 79.5 %collective-permute-done.8 = f32[512,2048]{1,0:T(8,128)} collective-permute-done((f32[512,2048]{1,0:T(8,128)}, f32[512,2048]{1,0:T(8,128)}, u32[]{:S(2)}, u32[]{:S(2)}) %collective-permute-start.8) | collective-permute-done | bytes 4194336 | tf_op jit(solution)/shard_map/gz_x/ppermute | solution.py:253
  680.2 85.0 %collective-permute-done.4 = f32[512,2048]{1,0:T(8,128)S(1)} collective-permute-done((f32[512,2048]{1,0:T(8,128)S(1)}, f32[512,2048]{1,0:T(8,128)S(1)}, u32[]{:S(2)}, u32[]{:S(2)}) %collective-permute-start.4) | collective-permute-done | bytes 4194336 | tf_op jit(solution)/shard_map/y_x/ppermute | solution.py:253
  770.7 158.7 %collective-permute-done.15 = bf16[1024,2048]{1,0:T(8,128)(2,1)} collective-permute-done((bf16[1024,2048]{1,0:T(8,128)(2,1)}, bf16[1024,2048]{1,0:T(8,128)(2,1)}, u32[]{:S(2)}, u32[]{:S(2)}) %collective-permute-start.15) | collective-permute-done | bytes 4194336 | tf_op jit(solution)/shard_map/gyo_y/ppermute | solution.py:253
  941.4 16.1 %convolution_convert_fusion = bf16[2048,1376]{0,1:T(8,128)(2,1)} fusion(bf16[2048,2048]{1,0:T(8,128)(2,1)} %constant_dynamic-update-slice_fusion.8, bf16[688,2048]{1,0:T(8,128)(2,1)S(1)} %copy-done.24, bf16[688,2048]{1,0:T(8,128)(2,1)S(1)} %copy-done.21), kind=kOutput, calls=%fused_computation.20 | convolution fusion | flops 11556814848 | bytes 19660800 | tf_op jit(solution)/shard_map/mlp2/dot_general | solution.py:27
  957.5 65.3 %collective-permute-done.13 = bf16[1024,2048]{1,0:T(8,128)(2,1)} collective-permute-done((bf16[1024,2048]{1,0:T(8,128)(2,1)}, bf16[1024,2048]{1,0:T(8,128)(2,1)}, u32[]{:S(2)}, u32[]{:S(2)}) %collective-permute-start.13) | collective-permute-done | bytes 4194336 | tf_op jit(solution)/shard_map/zo_y/ppermute | solution.py:253
  1031.6 9.7 fusion.49
  1041.3 7.8 fusion.51
  1051.5 16.8 %fusion.96 = f32[2048,1376]{0,1:T(8,128)} fusion(bf16[2048,2048]{1,0:T(8,128)(2,1)} %constant_dynamic-update-slice_fusion.10, bf16[2048,1376]{1,0:T(8,128)(2,1)S(1)} %bitcast.121), kind=kOutput, calls=%fused_computation.167 | convolution fusion | flops 11542724608 | bytes 25296896 | tf_op jit(solution)/shard_map/mlp2/dot_general | solution.py:23
  1068.3 22.2 %fusion.8 = (f32[2048,1376]{0,1:T(8,128)}, f32[2048,1376]{0,1:T(8,128)}) fusion(bf16[2048,2048]{1,0:T(8,128)(2,1)} %constant_dynamic-update-slice_fusion.10, bf16[2048,1376]{1,0:T(8,128)(2,1)} %bitcast.112), kind=kOutput, calls=%fused_computation.13 | convolution fusion | flops 11553996800 | bytes 36569088 | tf_op jit(solution)/shard_map/mlp2/dot_general | solution.py:23
  1090.4 9.7 convolution_convert_fusion.2.do_ref
  1100.1 60.6 %attn_bwd.1 = (bf16[4096,256]{1,0:T(8,128)(2,1)S(1)}, bf16[4096,256]{1,0:T(8,128)(2,1)S(1)}, bf16[4096,256]{1,0:T(8,128)(2,1)}) custom-call(s32[16]{0:T(128)S(1)} %and_select_fusion.lo_ref, bf16[4096,256]{1,0:T(8,128)(2,1)} %copy-done.5, bf16[4096,256]{1,0:T(8,128)(2,1)} %convolution_convert_fusion.2.do_ref, bf16[4096,256]{1,0:T(8,128)(2,1)} %copy-done, ...), custom_call_target="tpu_custom_call" | custom-call | flops 60000002048 | bytes 20000000 | tf_op jit(solution)/shard_map/attnb/attn_bwd/pallas_call | solution.py:227
  1167.2 17.4 %fusion.24 = f32[1024,1376]{0,1:T(8,128)} fusion(f32[1024,1376]{0,1:T(8,128)} %fusion.49, f32[2048,1376]{0,1:T(8,128)} %fusion.96, bf16[2048,1376]{0,1:T(8,128)(2,1)} %convolution_convert_fusion, f32[2048,1376]{0,1:T(8,128)} %get-tuple-element.126, bf16[2048,2048]{1,0:T(8,128)(2,1)} %constant_dynamic-update-slice_fusion.10, s32[]{:T(128)S(6)} %select_n.68), kind=kOutput, calls=%fused_computation.49 | convolution fusion | flops 5803769856 | bytes 43646980 | tf_op jit(solution)/shard_map/gwg/dot_general | solution.py:31
  1201.3 36.0 %collective-permute-done.9 = bf16[2048,768]{1,0:T(8,128)(2,1)} collective-permute-done((bf16[2048,768]{1,0:T(8,128)(2,1)}, bf16[2048,768]{1,0:T(8,128)(2,1)}, u32[]{:S(2)}, u32[]{:S(2)}) %collective-permute-start.9) | collective-permute-done | bytes 3145760 | tf_op jit(solution)/shard_map/doth/ppermute | solution.py:253
  1237.3 9.3 convolution_add_fusion
  1246.6 11.1 fusion.27
  1268.3 11.7 fusion.63
  1285.8 6.6 fusion.92
  1292.4 37.0 %all-to-all-done.9 = f32[4,256,1376]{1,2,0:T(8,128)} async-done(((f32[4,256,1376]{1,2,0:T(8,128)}), f32[4,256,1376]{1,2,0:T(8,128)}, u32[]{:S(2)}, u32[]{:S(2)}) %all-to-all-start.9) | async-done | bytes 5636128 | tf_op jit(solution)/shard_map/gwu/all_to_all | solution.py:378
  1332.7 9.7 fusion.93
  1342.4 9.1 fusion.66
  1351.5 7.7 all-to-all-done.5
  1361.6 9.6 add_add_fusion
  1378.6 9.8 fusion.94
  1391.9 14.5 convolution_add_fusion.3
  1411.9 6.2 copy.124
  1423.6 6.3 copy.125
  1430.0 9.5 fusion.95
  1451.6 48.8 %all-to-all-done.7 = f32[8,256,256]{2,1,0:T(8,128)} async-done(((f32[8,256,256]{2,1,0:T(8,128)}), f32[8,256,256]{2,1,0:T(8,128)}, u32[]{:S(2)}, u32[]{:S(2)}) %all-to-all-start.7) | async-done | bytes 2097184 | tf_op jit(solution)/shard_map/gwqkv/all_to_all | solution.py:412
  (240 shorter events, 219.9 us)
Async XLA Ops:
  7.2 187.7 %all-gather.5.cloned.1.call-start = ((), (), s32[]{:S(2)}) async-start(), calls=%async_computation.10 | async-start | bytes 18874368 | tf_op jit(solution)/shard_map/gx/all_gather | solution.py:250
  7.9 302.5 %all-gather.7.cloned.1.call-start = ((), (), s32[]{:S(2)}) async-start(), calls=%async_computation.11 | async-start | bytes 9437184 | tf_op jit(solution)/shard_map/gwo/all_gather | solution.py:250
  14.8 171.9 %all-to-all-start = ((bf16[256,8,768]{0,2,1:T(8,128)(2,1)}), bf16[256,8,768]{0,2,1:T(8,128)(2,1)}, u32[]{:S(2)}, u32[]{:S(2)}) async-start(bf16[256,8,768]{0,2,1:T(8,128)(2,1)} %bitcast.3), calls=%async_computation | async-start | bytes 6291456 | tf_op jit(solution)/shard_map/wqkv/all_to_all | solution.py:284
  19.1 274.1 %collective-permute-start.5 = (bf16[512,2048]{1,0:T(8,128)(2,1)}, bf16[512,2048]{1,0:T(8,128)(2,1)}, u32[]{:S(2)}, u32[]{:S(2)}) collective-permute-start(bf16[512,2048]{1,0:T(8,128)(2,1)} %param.15), channel_id=1, source_target_pairs={{0,2},{1,3},{2,0},{3,1},{4,6},{5,7},{6,4},{7,5}} | collective-permute-start | bytes 6291464 | tf_op jit(solution)/shard_map/gy_x/ppermute | solution.py:253
  186.7 90.4 %all-to-all-start.2 = ((bf16[256,8,1376]{0,2,1:T(8,128)(2,1)}), bf16[256,8,1376]{0,2,1:T(8,128)(2,1)}, u32[]{:S(2)}, u32[]{:S(2)}) async-start(bf16[256,8,1376]{0,2,1:T(8,128)(2,1)} %pad_maximum_fusion.1), calls=%async_computation.2 | async-start | bytes 11272192 | tf_op jit(solution)/shard_map/wg/all_to_all | solution.py:306
  223.7 35.0 %copy-start.5 = (bf16[4096,256]{1,0:T(8,128)(2,1)}, bf16[4096,256]{1,0:T(8,128)(2,1)S(1)}, u32[]{:S(2)}) copy-start(bf16[4096,256]{1,0:T(8,128)(2,1)S(1)} %get-tuple-element.22.q_ref) | copy-start | bytes 6291460
  223.7 35.1 %copy-start.6 = (bf16[4096,256]{1,0:T(8,128)(2,1)}, bf16[4096,256]{1,0:T(8,128)(2,1)S(1)}, u32[]{:S(2)}) copy-start(bf16[4096,256]{1,0:T(8,128)(2,1)S(1)} %get-tuple-element.23.k_ref) | copy-start | bytes 6291460
  223.7 35.1 %copy-start.8 = (bf16[256,4096]{1,0:T(8,128)(2,1)}, bf16[256,4096]{1,0:T(8,128)(2,1)S(1)}, u32[]{:S(2)}) copy-start(bf16[256,4096]{1,0:T(8,128)(2,1)S(1)} %get-tuple-element.27.kt_ref) | copy-start | bytes 6291460
  258.8 26.1 %copy-start = (bf16[4096,256]{1,0:T(8,128)(2,1)}, bf16[4096,256]{1,0:T(8,128)(2,1)S(1)}, u32[]{:S(2)}) copy-start(bf16[4096,256]{1,0:T(8,128)(2,1)S(1)} %get-tuple-element.25.o_ref) | copy-start | bytes 6291460
  277.1 29.8 %all-to-all-start.1 = ((bf16[8,512,256]{1,2,0:T(8,128)(2,1)}), bf16[8,512,256]{1,2,0:T(8,128)(2,1)}, u32[]{:S(2)}, u32[]{:S(2)}) async-start(bf16[8,512,256]{1,2,0:T(8,128)(2,1)} %copy.109), calls=%async_computation.1 | async-start | bytes 4194304 | tf_op jit(solution)/shard_map/oloc/all_to_all | solution.py:319
  280.4 39.2 %copy-start.31 = (f32[1,2,8,128]{3,1,2,0:T(2,128)}, f32[1,2,8,128]{3,1,2,0:T(2,128)S(1)}, u32[]{:S(2)}) copy-start(f32[1,2,8,128]{3,1,2,0:T(2,128)S(1)} %copy.133) | copy-start | bytes 24580
  299.8 156.3 %collective-permute-start.6 = (bf16[1024,2048]{1,0:T(8,128)(2,1)}, bf16[1024,2048]{1,0:T(8,128)(2,1)}, u32[]{:S(2)}, u32[]{:S(2)}) collective-permute-start(bf16[1024,2048]{1,0:T(8,128)(2,1)} %get-tuple-element.109), channel_id=1, source_target_pairs={{0,1},{1,0},{2,3},{3,2},{4,5},{5,4},{6,7},{7,6}} | collective-permute-start | bytes 12582920 | tf_op jit(solution)/shard_map/gy_s/ppermute | solution.py:253
  306.9 141.1 %all-to-all-start.3 = ((bf16[256,8,1376]{0,2,1:T(8,128)(2,1)}), bf16[256,8,1376]{0,2,1:T(8,128)(2,1)}, u32[]{:S(2)}, u32[]{:S(2)}) async-start(bf16[256,8,1376]{0,2,1:T(8,128)(2,1)} %pad_maximum_fusion.2), calls=%async_computation.3 | async-start | bytes 11272192 | tf_op jit(solution)/shard_map/wu/all_to_all | solution.py:306
  310.4 780.0 %all-gather.9.cloned.1.call-start = ((), (), s32[]{:S(2)}) async-start(), calls=%async_computation.12 | async-start | bytes 18874368 | tf_op jit(solution)/shard_map/ggh/all_gather | solution.py:250
  321.4 97.2 %collective-permute-start = (bf16[512,2048]{1,0:T(8,128)(2,1)S(1)}, bf16[512,2048]{1,0:T(8,128)(2,1)S(1)}, u32[]{:S(2)}, u32[]{:S(2)}) collective-permute-start(bf16[512,2048]{1,0:T(8,128)(2,1)S(1)} %fusion.40), channel_id=1, source_target_pairs={{0,2},{1,3},{2,0},{3,1},{4,6},{5,7},{6,4},{7,5}} | collective-permute-start | bytes 6291464 | tf_op jit(solution)/shard_map/z_x/ppermute | solution.py:253
  323.3 110.8 %collective-permute-start.2 = (bf16[688,2048]{1,0:T(8,128)(2,1)}, bf16[688,2048]{1,0:T(8,128)(2,1)}, u32[]{:S(2)}, u32[]{:S(2)}) collective-permute-start(bf16[688,2048]{1,0:T(8,128)(2,1)} %param.24), channel_id=1, source_target_pairs={{0,4},{1,5},{2,6},{3,7},{4,0},{5,1},{6,2},{7,3}} | collective-permute-start | bytes 8454152 | tf_op jit(solution)/shard_map/wd/ppermute | solution.py:253
  422.5 54.6 %collective-permute-start.1 = (bf16[1024,2048]{1,0:T(8,128)(2,1)}, bf16[1024,2048]{1,0:T(8,128)(2,1)}, u32[]{:S(2)}, u32[]{:S(2)}) collective-permute-start(bf16[1024,2048]{1,0:T(8,128)(2,1)} %pad_maximum_fusion.4), channel_id=1, source_target_pairs={{0,1},{1,0},{2,3},{3,2},{4,5},{5,4},{6,7},{7,6}} | collective-permute-start | bytes 12582920 | tf_op jit(solution)/shard_map/z_s/ppermute | solution.py:253
  523.2 25.2 %slice-start.4 = ((s8[5636096]{0:T(1024)(128)(4,1)}), s8[4194304]{0:T(1024)(128)(4,1)S(1)}, s32[]{:S(2)}) async-start(s8[5636096]{0:T(1024)(128)(4,1)} %bitcast.148), calls=%async_computation.17 | async-start | bytes 8388608
  523.2 35.0 %slice-start = ((s8[5767168]{0:T(1024)(128)(4,1)}), s8[4194304]{0:T(1024)(128)(4,1)S(1)}, s32[]{:S(2)}) async-start(s8[5767168]{0:T(1024)(128)(4,1)} %bitcast.113), calls=%async_computation.13 | async-start | bytes 8388608
  535.2 23.0 %slice-start.1 = ((s8[5767168]{0:T(1024)(128)(4,1)}), s8[1572864]{0:T(1024)(128)(4,1)S(1)}, s32[]{:S(2)}) async-start(s8[5767168]{0:T(1024)(128)(4,1)} %bitcast.113), calls=%async_computation.14 | async-start | bytes 3145728
  548.4 18.9 %collective-permute-start.7 = (f32[1024,2048]{1,0:T(8,128)}, f32[1024,2048]{1,0:T(8,128)}, u32[]{:S(2)}, u32[]{:S(2)}) collective-permute-start(f32[1024,2048]{1,0:T(8,128)} %convolution_add_fusion.1), channel_id=1, source_target_pairs={{0,1},{1,0},{2,3},{3,2},{4,5},{5,4},{6,7},{7,6}} | collective-permute-start | bytes 25165832 | tf_op jit(solution)/shard_map/gz_s/ppermute | solution.py:253
  557.7 26.4 %collective-permute-start.3 = (f32[1024,2048]{1,0:T(8,128)}, f32[1024,2048]{1,0:T(8,128)}, u32[]{:S(2)}, u32[]{:S(2)}) collective-permute-start(f32[1024,2048]{1,0:T(8,128)} %fusion.60), channel_id=1, source_target_pairs={{0,1},{1,0},{2,3},{3,2},{4,5},{5,4},{6,7},{7,6}} | collective-permute-start | bytes 25165832 | tf_op jit(solution)/shard_map/y_s/ppermute | solution.py:253
  582.9 93.4 %collective-permute-start.8 = (f32[512,2048]{1,0:T(8,128)}, f32[512,2048]{1,0:T(8,128)}, u32[]{:S(2)}, u32[]{:S(2)}) collective-permute-start(f32[512,2048]{1,0:T(8,128)} %slice.97), channel_id=1, source_target_pairs={{0,2},{1,3},{2,0},{3,1},{4,6},{5,7},{6,4},{7,5}} | collective-permute-start | bytes 12582920 | tf_op jit(solution)/shard_map/gz_x/ppermute | solution.py:253
  595.4 80.9 %copy-start.13 = (bf16[512,2048]{1,0:T(8,128)(2,1)S(1)}, bf16[512,2048]{1,0:T(8,128)(2,1)}, u32[]{:S(2)}) copy-start(bf16[512,2048]{1,0:T(8,128)(2,1)} %copy-done.12) | copy-start | bytes 6291460
  595.4 80.9 %copy-start.32 = (f32[1,2,8,128]{3,1,2,0:T(2,128)S(1)}, f32[1,2,8,128]{3,1,2,0:T(2,128)}, u32[]{:S(2)}) copy-start(f32[1,2,8,128]{3,1,2,0:T(2,128)} %copy-done.31) | copy-start | bytes 24580
  595.4 80.9 %copy-start.34 = (f32[512]{0:T(512)S(1)}, f32[512]{0:T(512)}, u32[]{:S(2)}) copy-start(f32[512]{0:T(512)} %copy-done.33) | copy-start | bytes 6148
  596.0 169.3 %collective-permute-start.4 = (f32[512,2048]{1,0:T(8,128)S(1)}, f32[512,2048]{1,0:T(8,128)S(1)}, u32[]{:S(2)}, u32[]{:S(2)}) collective-permute-start(f32[512,2048]{1,0:T(8,128)S(1)} %slice.91), channel_id=1, source_target_pairs={{0,2},{1,3},{2,0},{3,1},{4,6},{5,7},{6,4},{7,5}} | collective-permute-start | bytes 12582920 | tf_op jit(solution)/shard_map/y_x/ppermute | solution.py:253
  770.3 159.1 %collective-permute-start.15 = (bf16[1024,2048]{1,0:T(8,128)(2,1)}, bf16[1024,2048]{1,0:T(8,128)(2,1)}, u32[]{:S(2)}, u32[]{:S(2)}) collective-permute-start(bf16[1024,2048]{1,0:T(8,128)(2,1)} %get-tuple-element.109), channel_id=1, source_target_pairs={{0,4},{1,5},{2,6},{3,7},{4,0},{5,1},{6,2},{7,3}} | collective-permute-start | bytes 12582920 | tf_op jit(solution)/shard_map/gyo_y/ppermute | solution.py:253
  929.4 7.1 collective-permute-start.16
  929.4 93.4 %collective-permute-start.13 = (bf16[1024,2048]{1,0:T(8,128)(2,1)}, bf16[1024,2048]{1,0:T(8,128)(2,1)}, u32[]{:S(2)}, u32[]{:S(2)}) collective-permute-start(bf16[1024,2048]{1,0:T(8,128)(2,1)} %pad_maximum_fusion.4), channel_id=1, source_target_pairs={{0,4},{1,5},{2,6},{3,7},{4,0},{5,1},{6,2},{7,3}} | collective-permute-start | bytes 12582920 | tf_op jit(solution)/shard_map/zo_y/ppermute | solution.py:253
  929.7 271.5 %collective-permute-start.10 = (bf16[2048,768]{1,0:T(8,128)(2,1)}, bf16[2048,768]{1,0:T(8,128)(2,1)}, u32[]{:S(2)}, u32[]{:S(2)}) collective-permute-start(bf16[2048,768]{1,0:T(8,128)(2,1)} %bitcast.128), channel_id=1, source_target_pairs={{0,4},{1,5},{2,6},{3,7},{4,0},{5,1},{6,2},{7,3}} | collective-permute-start | bytes 9437192 | tf_op jit(solution)/shard_map/woth/ppermute | solution.py:253
  957.5 70.2 %copy-start.17 = (bf16[512,2048]{1,0:T(8,128)(2,1)S(1)}, bf16[512,2048]{1,0:T(8,128)(2,1)}, u32[]{:S(2)}) copy-start(bf16[512,2048]{1,0:T(8,128)(2,1)} %copy-done.16) | copy-start | bytes 6291460
  1022.8 26.3 %collective-permute-start.14 = (bf16[1024,2048]{1,0:T(8,128)(2,1)}, bf16[1024,2048]{1,0:T(8,128)(2,1)S(1)}, u32[]{:S(2)}, u32[]{:S(2)}) collective-permute-start(bf16[1024,2048]{1,0:T(8,128)(2,1)} %collective-permute-done.13), channel_id=1, source_target_pairs={{0,1},{1,0},{2,3},{3,2},{4,5},{5,4},{6,7},{7,6}} | collective-permute-start | bytes 12582920 | tf_op jit(solution)/shard_map/zo_ys/ppermute | solution.py:253
  1031.6 19.8 %slice-start.2 = ((s8[5767168]{0:T(1024)(128)(4,1)}), s8[4194304]{0:T(1024)(128)(4,1)S(1)}, s32[]{:S(2)}) async-start(s8[5767168]{0:T(1024)(128)(4,1)} %bitcast.119), calls=%async_computation.15 | async-start | bytes 8388608
  1068.3 22.2 %copy-start.28 = (bf16[2,128,2048]{2,1,0:T(8,128)(2,1)S(1)}, bf16[2,128,2048]{2,1,0:T(8,128)(2,1)}, u32[]{:S(2)}) copy-start(bf16[2,128,2048]{2,1,0:T(8,128)(2,1)} %param.20) | copy-start | bytes 3145732
  1166.8 70.5 %collective-permute-start.9 = (bf16[2048,768]{1,0:T(8,128)(2,1)}, bf16[2048,768]{1,0:T(8,128)(2,1)}, u32[]{:S(2)}, u32[]{:S(2)}) collective-permute-start(bf16[2048,768]{1,0:T(8,128)(2,1)} %pad_maximum_fusion.6), channel_id=1, source_target_pairs={{0,4},{1,5},{2,6},{3,7},{4,0},{5,1},{6,2},{7,3}} | collective-permute-start | bytes 9437192 | tf_op jit(solution)/shard_map/doth/ppermute | solution.py:253
  1190.2 70.5 %all-to-all-start.8 = ((f32[4,256,1376]{1,2,0:T(8,128)}), f32[4,256,1376]{1,2,0:T(8,128)}, u32[]{:S(2)}, u32[]{:S(2)}) async-start(f32[4,256,1376]{1,2,0:T(8,128)} %bitcast.102), calls=%async_computation.8 | async-start | bytes 11272192 | tf_op jit(solution)/shard_map/gwg/all_to_all | solution.py:378
  1195.3 51.3 %slice-start.12 = ((s8[5636096]{0:T(1024)(128)(4,1)}), s8[4194304]{0:T(1024)(128)(4,1)S(1)}, s32[]{:S(2)}) async-start(s8[5636096]{0:T(1024)(128)(4,1)} %bitcast.154), calls=%async_computation.25 | async-start | bytes 8388608
  1201.3 45.3 %slice-start.13 = ((s8[5636096]{0:T(1024)(128)(4,1)}), s8[1441792]{0:T(1024)(128)(4,1)S(1)}, s32[]{:S(2)}) async-start(s8[5636096]{0:T(1024)(128)(4,1)} %bitcast.154), calls=%async_computation.26 | async-start | bytes 2883584
  1246.6 115.0 %collective-permute-start.11 = (f32[1024,2048]{1,0:T(8,128)}, f32[1024,2048]{1,0:T(8,128)}, u32[]{:S(2)}, u32[]{:S(2)}) collective-permute-start(f32[1024,2048]{1,0:T(8,128)} %convolution_add_fusion), channel_id=1, source_target_pairs={{0,1},{1,0},{2,3},{3,2},{4,5},{5,4},{6,7},{7,6}} | collective-permute-start | bytes 25165832 | tf_op jit(solution)/shard_map/gu_s/ppermute | solution.py:253
  1260.7 68.8 %all-to-all-start.9 = ((f32[4,256,1376]{1,2,0:T(8,128)}), f32[4,256,1376]{1,2,0:T(8,128)}, u32[]{:S(2)}, u32[]{:S(2)}) async-start(f32[4,256,1376]{1,2,0:T(8,128)} %bitcast.101), calls=%async_computation.9 | async-start | bytes 11272192 | tf_op jit(solution)/shard_map/gwu/all_to_all | solution.py:378
  1329.4 29.8 %all-to-all-start.5 = ((f32[8,256,256]{2,1,0:T(8,128)}), f32[8,256,256]{2,1,0:T(8,128)}, u32[]{:S(2)}, u32[]{:S(2)}) async-start(f32[8,256,256]{2,1,0:T(8,128)} %bitcast.134), calls=%async_computation.5 | async-start | bytes 4194304 | tf_op jit(solution)/shard_map/gwqkv/all_to_all | solution.py:412
  1359.2 29.2 %all-to-all-start.6 = ((f32[8,256,256]{2,1,0:T(8,128)}), f32[8,256,256]{2,1,0:T(8,128)S(1)}, u32[]{:S(2)}, u32[]{:S(2)}) async-start(f32[8,256,256]{2,1,0:T(8,128)} %bitcast.133), calls=%async_computation.6 | async-start | bytes 4194304 | tf_op jit(solution)/shard_map/gwqkv/all_to_all | solution.py:412
  1376.7 130.5 %collective-permute-start.12 = (f32[512,2048]{1,0:T(8,128)}, f32[512,2048]{1,0:T(8,128)}, u32[]{:S(2)}, u32[]{:S(2)}) collective-permute-start(f32[512,2048]{1,0:T(8,128)} %slice.101), channel_id=1, source_target_pairs={{0,2},{1,3},{2,0},{3,1},{4,6},{5,7},{6,4},{7,5}} | collective-permute-start | bytes 12582920 | tf_op jit(solution)/shard_map/gu_x/ppermute | solution.py:253
  1388.5 17.9 %copy-start.14 = (f32[8,256,256]{2,1,0:T(8,128)}, f32[8,256,256]{2,1,0:T(8,128)S(1)}, u32[]{:S(2)}) copy-start(f32[8,256,256]{2,1,0:T(8,128)S(1)} %all-to-all-done.6) | copy-start | bytes 6291460
  1388.5 112.0 %all-to-all-start.7 = ((f32[8,256,256]{2,1,0:T(8,128)}), f32[8,256,256]{2,1,0:T(8,128)}, u32[]{:S(2)}, u32[]{:S(2)}) async-start(f32[8,256,256]{2,1,0:T(8,128)} %bitcast.132), calls=%async_computation.7 | async-start | bytes 4194304 | tf_op jit(solution)/shard_map/gwqkv/all_to_all | solution.py:412
  1448.9 58.3 %copy-start.11 = (bf16[512,2048]{1,0:T(8,128)(2,1)S(1)}, bf16[512,2048]{1,0:T(8,128)(2,1)}, u32[]{:S(2)}) copy-start(bf16[512,2048]{1,0:T(8,128)(2,1)} %param.13) | copy-start | bytes 6291460
  1513.1 7.1 all-to-all-start.4
  (37 other events, 285.8 us)
Sparse Core Ops, SparseCore 0:
  9.8 160.2 all-gather.4
  171.9 86.3 all-gather.6
  770.4 152.1 all-gather.8
